TPU v7x, 32 devices: a whole 2x2x4 slice. The times are simulated.
32 devices in a mesh: dp: 4 (over z), seq: 8 (over y, x, core).
Axes of the slice: x: 2, y: 2, z: 4, core: 2. Of those that a mesh axis runs over, the one named last changes fastest.
Arguments:
- projections: bfloat16 [1, 4, 1024, 4096], P(None, 'dp', 'seq'), may hold values from -6 to 6
- rotated_query_gradient: bfloat16 [1, 4, 1024, 4096], P(None, 'dp', None, 'seq'), may hold values from -6 to 6
- gains: float32 [1, 4096], replicated, may hold values from 0.25 to 1.75
- adapter_lowering: bfloat16 [1, 48, 5120], P(None, 'dp'), may hold values from -0.078125 to 0.078125
- adapter_raising: bfloat16 [1, 48, 4096], P(None, 'dp'), may hold values from -0.875 to 0.875
- activations: bfloat16 [4, 1024, 5120], P('dp', 'seq'), may hold values from -6 to 6
- positions: int32 [3, 4, 1024], P(None, 'dp', 'seq'), may hold values from 0 to 22, as said below
- valid: int32 [4, 1024], P('dp', 'seq'), may hold values from 0 to 1, as said below
Outputs:
- grad_down: float32 [1, 48, 5120], P(None, 'dp')
- grad_up: float32 [1, 48, 4096], P(None, 'dp')
- grad_gain: float32 [1, 4096], replicated
Inputs may be any that keep to these rules, and one draw needn't show every extreme that they name: `positions`: within a video the frame index never falls; one frame holds 128 tokens. Every eighth token of a video is valid.
All inputs are finite; a program needn't handle non-finite values.
Results may differ from a plain program's by a relative error of at most 0.0041.
Values may be sent and summed in bfloat16 or wider, within the bound.
A program may use at most 64 MiB of HBM per device.

v0:
```python
import functools

import jax
import jax.numpy as jnp
import numpy as np
from jax import lax
from jax.experimental import pallas as pl
from jax.experimental.pallas import tpu as pltpu
from jax.sharding import PartitionSpec as P

HD = 128
EPSILON = 1e-06
LANES = 128
BF = jnp.bfloat16
F32 = jnp.float32
MESH = pl.DeviceIdType.MESH
NT = (((1,), (1,)), ((), ()))


def group_counts():
    one_sixth = HD // 6
    return (HD // 2 - 2 * one_sixth, one_sixth, one_sixth)


def lane_frequencies():
    pieces = []
    for n in group_counts():
        pieces.append(np.float32(10000.0) ** (-np.arange(n, dtype=np.float32) / np.float32(n)))
    return np.repeat(np.concatenate(pieces).astype(np.float32), 2)[None]


def kernel(
    cfg,
    proj_hbm, cot_hbm, act_hbm, low_hbm, rai_hbm, gains_ref, freq_ref, pos_ref, valid_ref,
    down_ref, up_ref, gain_ref,
    proj, act, cot, cot_src, low, rai, fold, packed, adapt, scaled, back_acc, dot_acc, inv_ref, cos_ref, sin_ref, redt, backt,
    small_send, small_recv, small_dp, small_dp_recv, small_fin, small_ag,
    d2d_send_u, d2d_recv_u, own_u, rs_send_u, rs_recv_u, tot_u, dp_send_u, dp_f_u, dp_recv_u, ag_u, fin_u,
    d2d_send_d, d2d_recv_d, own_d, rs_send_d, rs_recv_d, tot_d, dp_send_d, dp_f_d, dp_recv_d, ag_d, fin_d,
    local_sem, cot_s, cot_r, ad_s, ad_r, rel_s, rel_r,
    sm_s, sm_r, smd_s, smd_r, sma_s, sma_r,
    d2d_s, d2d_r, rs_s, rs_r, dp_s, dp_r, ag_s, ag_r,
):
    S, D, T, F, W, R, RP, LH, UH, M, QF, fd = (
        cfg[k] for k in ("S", "D", "T", "F", "W", "R", "RP", "LH", "UH", "M", "QF", "fd")
    )
    K = S // 2
    ranks = D * R
    hw = 256 if F % 256 == 0 else 128
    d = lax.axis_index("dp")
    s = lax.axis_index("seq")
    c = lax.rem(s, 2)
    chip = s // 2
    sib = s + 1 - 2 * c

    def copy(src, dst, ss, rs, dp, seq):
        return pltpu.make_async_remote_copy(
            src_ref=src, dst_ref=dst, send_sem=ss, recv_sem=rs,
            device_id=(dp, seq), device_id_type=MESH,
        )

    loads = [
        pltpu.make_async_copy(proj_hbm, proj, local_sem.at[0]),
        pltpu.make_async_copy(act_hbm, act.at[:, pl.ds(0, M)], local_sem.at[1]),
        pltpu.make_async_copy(cot_hbm, cot_src, local_sem.at[2]),
        pltpu.make_async_copy(low_hbm, low, local_sem.at[3]),
        pltpu.make_async_copy(rai_hbm, rai, local_sem.at[4]),
    ]
    for i in (3, 4, 2, 0, 1):
        loads[i].start()

    barrier = pltpu.get_barrier_semaphore()
    for k in range(1, S):
        pl.semaphore_signal(barrier, inc=1, device_id=(d, lax.rem(s + k, S)), device_id_type=MESH)
    for k in range(1, D):
        pl.semaphore_signal(barrier, inc=1, device_id=(lax.rem(d + k, D), s), device_id_type=MESH)

    LF, UF = LH // fd, UH // fd
    fold[...] = jnp.zeros_like(fold)
    loads[3].wait()
    loads[4].wait()
    for h in range(2):
        for q in range(fd):
            fold[q * R:(q + 1) * R, 0:LF] = low[:, h * LH + q * LF:h * LH + (q + 1) * LF].astype(F32)
            fold[q * R:(q + 1) * R, LF:LF + UF] = rai[:, h * UH + q * UF:h * UH + (q + 1) * UF].astype(F32)
        packed[d, h] = fold[0:packed.shape[2], :].astype(BF)

    loads[2].wait()
    pl.semaphore_wait(barrier, S + D - 2)

    def cot_copy(peer, slot):
        return copy(cot_src.at[peer], cot.at[slot], cot_s.at[peer], cot_r.at[slot], d, peer)

    def adapt_copy(peer, slot):
        return copy(packed.at[d, c], packed.at[slot, c], ad_s.at[peer], ad_r.at[slot], peer, s)

    def relay_copy(slot, half):
        return copy(packed.at[slot, half], packed.at[slot, half], rel_s.at[slot], rel_r.at[slot], d, sib)

    for k in range(1, D):
        adapt_copy(lax.rem(d + k, D), d).start()
    for k in range(1, S):
        cot_copy(lax.rem(s + k, S), s).start()

    n0, n1, _ = group_counts()
    lane = lax.broadcasted_iota(jnp.int32, (T, LANES), 1)

    def column(row):
        return jnp.broadcast_to(row.astype(F32), (LANES, T)).T

    index = jnp.where(
        lane < 2 * n0, column(pos_ref[0]),
        jnp.where(lane < 2 * (n0 + n1), column(pos_ref[1]), column(pos_ref[2])),
    )
    angle = index * freq_ref[...]
    ok = column(valid_ref[...])
    co = jnp.cos(angle) * ok
    si = jnp.sin(angle) * ok
    for i in range(hw // LANES):
        cos_ref[:, i * LANES:(i + 1) * LANES] = co
        sin_ref[:, i * LANES:(i + 1) * LANES] = si
    row_i = lax.broadcasted_iota(jnp.int32, (hw, hw), 0)
    col_i = lax.broadcasted_iota(jnp.int32, (hw, hw), 1)
    even = lax.rem(col_i, 2) == 0
    swap = jnp.where(
        even & (row_i == col_i + 1), 1.0, jnp.where(jnp.logical_not(even) & (row_i == col_i - 1), -1.0, 0.0)
    ).astype(BF)
    count = jnp.sum(valid_ref[...].astype(F32), axis=1, keepdims=True)
    small_send[...] = jnp.broadcast_to(count[:, :, None], small_send.shape)

    loads[0].wait()
    square = jnp.zeros((T, LANES), F32)
    for i in range(QF // LANES):
        v = proj[:, i * LANES:(i + 1) * LANES].astype(F32)
        square += v * v
    inverse = lax.rsqrt(jnp.sum(square, axis=1, keepdims=True) / QF + EPSILON)
    inv_ref[...] = jnp.broadcast_to(inverse, (T, LANES))
    dot_acc[...] = jnp.zeros_like(dot_acc)

    def wide(x):
        return jnp.concatenate([x] * (hw // LANES), axis=1) if hw > LANES else x

    def chunk(p, source=cot):
        inv = wide(inv_ref[...])
        cw, sw = cos_ref[...], sin_ref[...]
        for i in range(F // hw):
            cols = pl.ds(pl.multiple_of(p * F + i * hw, LANES), hw)
            x = source[p, :, i * hw:(i + 1) * hw]
            xs = jnp.dot(x, swap, preferred_element_type=F32)
            un = cw * x.astype(F32) + sw * xs
            prod = un * (proj[:, cols].astype(F32) * inv)
            g = jnp.sum(prod, axis=0, keepdims=True)
            for t in range(hw // LANES):
                j = i * (hw // LANES) + t
                small_send[p, j:j + 1, :] = g[:, t * LANES:(t + 1) * LANES]
            gn = gains_ref[:, cols]
            scaled[p, :, i * hw:(i + 1) * hw] = un * gn
            pg = prod * gn
            acc = pg[:, :LANES]
            for t in range(1, hw // LANES):
                acc += pg[:, t * LANES:(t + 1) * LANES]
            dot_acc[...] += acc

    chunk(s, cot_src)
    cot_copy(sib, sib).wait_recv()
    chunk(sib)

    def rest(j, carry):
        p = lax.rem(2 * chip + 2 + j, S)
        cot_copy(p, p).wait_recv()
        chunk(p)
        return carry

    half_rest = (S - 2) // 2
    lax.fori_loop(0, half_rest, rest, 0)
    for k in range(1, D):
        e = lax.rem(d + k, D)
        adapt_copy(e, e).wait_recv()
        relay_copy(e, c).start()
    lax.fori_loop(half_rest, S - 2, rest, 0)

    def small_copy(peer, slot):
        return copy(small_send.at[peer], small_recv.at[slot], sm_s.at[peer], sm_r.at[slot], d, peer)

    for k in range(1, S):
        small_copy(lax.rem(s + k, S), s).start()

    r_i = lax.broadcasted_iota(jnp.int32, (ranks, D * RP), 0)
    q_i = lax.broadcasted_iota(jnp.int32, (ranks, D * RP), 1)
    pick = jnp.where(q_i == (r_i // R) * RP + lax.rem(r_i, R), 1.0, 0.0).astype(BF)

    def dense_transposed(x):
        return lax.dot_general(pick, x.astype(BF), NT, preferred_element_type=F32).astype(BF)

    for k in range(1, D):
        e = lax.rem(d + k, D)
        relay_copy(e, 1 - c).wait_recv()

    def unfold(e, carry):
        for h in range(2):
            fold[0:packed.shape[2], :] = packed[e, h].astype(F32)
            for q in range(fd):
                rows = fold[q * R:q * R + RP, :].astype(BF)
                adapt[e, h, :, q * LF:(q + 1) * LF] = rows[:, 0:LF]
                adapt[e, h, :, LH + q * UF:LH + (q + 1) * UF] = rows[:, LF:LF + UF]
        return carry

    lax.fori_loop(0, D, unfold, 0)
    loads[1].wait()
    red = jnp.zeros((T, D * RP), F32)
    for h in range(2):
        lowering = adapt[:, h, :, 0:LH].reshape(D * RP, LH)
        red += lax.dot_general(act[:, h * LH:(h + 1) * LH], lowering, NT, preferred_element_type=F32)
    redt[...] = dense_transposed(red)

    back_acc[...] = jnp.zeros_like(back_acc)
    dot_mean = jnp.sum(dot_acc[...], axis=1, keepdims=True) / QF
    mean_w = jnp.broadcast_to(dot_mean, (T, LANES))
    dot_acc[...] = mean_w

    def up_term(p):
        inv = wide(inv_ref[...])
        mean = wide(dot_acc[...])
        parts = []
        for i in range(F // hw):
            cols = pl.ds(pl.multiple_of(p * F + i * hw, LANES), hw)
            nrm = proj[:, cols].astype(F32) * inv
            parts.append((inv * (scaled[p, :, i * hw:(i + 1) * hw] - nrm * mean)).astype(BF))
        delta = jnp.concatenate(parts, axis=1) if len(parts) > 1 else parts[0]
        h = p // K
        off = pl.multiple_of(LH + lax.rem(p, K) * F, LANES)
        raising = adapt[:, h, :, pl.ds(off, F)].reshape(D * RP, F)
        back_acc[...] += lax.dot_general(delta, raising, NT, preferred_element_type=F32)
        return jnp.dot(redt[...], delta, preferred_element_type=F32)

    def down_term(p):
        cols = pl.ds(pl.multiple_of(p * W, LANES), W)
        return jnp.dot(backt[...], act[:, cols], preferred_element_type=F32)

    up = dict(i=0, term=up_term, d2d_send=d2d_send_u, d2d_recv=d2d_recv_u, own=own_u,
              rs_send=rs_send_u, rs_recv=rs_recv_u, tot=tot_u, dp_send=dp_send_u, dp_f=dp_f_u,
              dp_recv=dp_recv_u, ag=ag_u, fin=fin_u, out=up_ref, width=F)
    down = dict(i=1, term=down_term, d2d_send=d2d_send_d, d2d_recv=d2d_recv_d, own=own_d,
                rs_send=rs_send_d, rs_recv=rs_recv_d, tot=tot_d, dp_send=dp_send_d, dp_f=dp_f_d,
                dp_recv=dp_recv_d, ag=ag_d, fin=fin_d, out=down_ref, width=W)

    def d2d_copy(b, k):
        i = b["i"]
        return copy(b["d2d_send"].at[k], b["d2d_recv"].at[k], d2d_s.at[i, k], d2d_r.at[i, k], d, sib)

    def rs_copy(b, peer, slot):
        i = b["i"]
        return copy(b["rs_send"].at[peer], b["rs_recv"].at[slot], rs_s.at[i, peer], rs_r.at[i, slot],
                    d, 2 * peer + c)

    def dp_copy(b, peer, slot):
        i = b["i"]
        return copy(b["dp_send"].at[peer], b["dp_recv"].at[slot], dp_s.at[i, peer], dp_r.at[i, slot],
                    peer, s)

    def ag_copy(b, peer, slot):
        i = b["i"]
        return copy(b["fin"], b["ag"].at[slot], ag_s.at[i, peer], ag_r.at[i, slot], d, peer)

    def scatter(b):
        def for_sibling(j, carry):
            k = lax.rem(chip + 1 + j, K)
            b["d2d_send"][k] = b["term"](2 * k + 1 - c).astype(BF)
            d2d_copy(b, k).start()
            return carry

        def for_this_core(j, carry):
            k = lax.rem(chip + 1 + j, K)
            b["own"][k] = b["term"](2 * k + c)
            return carry

        lax.fori_loop(0, K, for_sibling, 0)
        lax.fori_loop(0, K, for_this_core, 0)
        for j in range(1, K):
            k = lax.rem(chip + j, K)
            d2d_copy(b, k).wait_recv()
            b["rs_send"][k] = (b["own"][k] + b["d2d_recv"][k].astype(F32)).astype(BF)
            rs_copy(b, k, chip).start()

    def dp_stage(b):
        d2d_copy(b, chip).wait_recv()
        total = b["own"][chip] + b["d2d_recv"][chip].astype(F32)
        for j in range(1, K):
            q = lax.rem(chip + j, K)
            rs_copy(b, q, q).wait_recv()
            total += b["rs_recv"][q].astype(F32)
        b["tot"][0:ranks, :] = total
        for e in range(D):
            rows = b["tot"][e * R:e * R + RP, :]
            b["dp_f"][e] = rows
            b["dp_send"][e] = rows.astype(BF)
        for k in range(1, D):
            dp_copy(b, lax.rem(d + k, D), d).start()

    def gather(b, factor):
        total = b["dp_f"][d]
        for k in range(1, D):
            e = lax.rem(d + k, D)
            dp_copy(b, e, e).wait_recv()
            total += b["dp_recv"][e].astype(F32)
        fin = (total * factor).astype(BF)
        b["fin"][...] = fin
        for k in range(1, S):
            ag_copy(b, lax.rem(s + k, S), s).start()
        cols = pl.ds(pl.multiple_of(s * b["width"], LANES), b["width"])
        b["out"][:, cols] = fin.astype(F32)[0:R]

    scatter(up)

    small = small_send[s]
    for k in range(1, S):
        q = lax.rem(s + k, S)
        small_copy(q, q).wait_recv()
        small += small_recv[q]
    small_dp[...] = small

    def small_dp_copy(peer, slot):
        return copy(small_dp, small_dp_recv.at[slot], smd_s.at[peer], smd_r.at[slot], peer, s)

    for k in range(1, D):
        small_dp_copy(lax.rem(d + k, D), d).start()

    backt[...] = dense_transposed(back_acc[...])
    scatter(down)
    dp_stage(up)

    small = small_dp[...]
    for k in range(1, D):
        e = lax.rem(d + k, D)
        small_dp_copy(e, e).wait_recv()
        small += small_dp_recv[e]
    groups = F // LANES
    factor = F32(cfg["tokens"]) / small[groups:groups + 1, 0:1]
    small_fin[...] = small * factor

    def small_ag_copy(peer, slot):
        return copy(small_fin, small_ag.at[slot], sma_s.at[peer], sma_r.at[slot], d, peer)

    for k in range(1, S):
        small_ag_copy(lax.rem(s + k, S), s).start()

    dp_stage(down)
    gather(up, factor)
    gather(down, factor)

    def put_gain(q, value):
        for j in range(groups):
            cols = pl.ds(pl.multiple_of(q * F + j * LANES, LANES), LANES)
            gain_ref[:, cols] = value[j:j + 1, :]

    put_gain(s, small_fin[...])
    for k in range(1, S):
        q = lax.rem(s + k, S)
        small_ag_copy(q, q).wait_recv()
        put_gain(q, small_ag[q])
    for b in (up, down):
        for k in range(1, S):
            q = lax.rem(s + k, S)
            ag_copy(b, q, q).wait_recv()
            cols = pl.ds(pl.multiple_of(q * b["width"], LANES), b["width"])
            b["out"][:, cols] = b["ag"][q].astype(F32)[0:R]

    for k in range(1, D):
        e = lax.rem(d + k, D)
        adapt_copy(e, d).wait_send()
        relay_copy(e, c).wait_send()
        small_dp_copy(e, d).wait_send()
        for b in (up, down):
            dp_copy(b, e, d).wait_send()
    for k in range(1, S):
        q = lax.rem(s + k, S)
        cot_copy(q, s).wait_send()
        small_copy(q, s).wait_send()
        small_ag_copy(q, s).wait_send()
        for b in (up, down):
            ag_copy(b, q, s).wait_send()
    for b in (up, down):
        d2d_copy(b, chip).wait_send()
        for j in range(1, K):
            k = lax.rem(chip + j, K)
            d2d_copy(b, k).wait_send()
            rs_copy(b, k, chip).wait_send()


def place(down_ref, up_ref, gain_ref, down_out, up_out, gain_out):
    for r in range(down_out.shape[0]):
        down_out[r] = down_ref[r:r + 1, 0:down_out.shape[2]]
        up_out[r] = up_ref[r:r + 1, :]
    gain_out[...] = gain_ref[...]


def shards(projections, rotated_query_gradient, gains, adapter_lowering, adapter_raising,
           activations, positions, valid):
    D, S = lax.axis_size("dp"), lax.axis_size("seq")
    T, QF = projections.shape[2:]
    F = rotated_query_gradient.shape[3]
    R, M = adapter_lowering.shape[1:]
    W = -(-M // (LANES * S)) * LANES
    RP = -(-R // 16) * 16
    LH, UH = M // 2, QF // 2
    K = S // 2
    ranks = D * R
    fd = 4 if R % 4 == 0 and LH % (4 * LANES) == 0 and UH % (4 * LANES) == 0 else 1
    folded = -(-fd * R // 16) * 16
    cfg = dict(S=S, D=D, T=T, F=F, W=W, R=R, RP=RP, LH=LH, UH=UH, M=M, QF=QF, fd=fd, tokens=D * S * T)

    def stage(width):
        return [
            pltpu.VMEM((K, ranks, width), BF),
            pltpu.VMEM((K, ranks, width), BF),
            pltpu.VMEM((K, ranks, width), F32),
            pltpu.VMEM((K, ranks, width), BF),
            pltpu.VMEM((K, ranks, width), BF),
            pltpu.VMEM((ranks + RP, width), F32),
            pltpu.VMEM((D, RP, width), BF),
            pltpu.VMEM((D, RP, width), F32),
            pltpu.VMEM((D, RP, width), BF),
            pltpu.VMEM((S, RP, width), BF),
            pltpu.VMEM((RP, width), BF),
        ]

    hw = 256 if F % 256 == 0 else 128
    dma = pltpu.SemaphoreType.DMA
    any_space = pl.BlockSpec(memory_space=pl.ANY)
    vmem = pl.BlockSpec(memory_space=pltpu.VMEM)
    small_rows = -(-(F // LANES + 1) // 8) * 8
    down, up, gain = pl.pallas_call(
        functools.partial(kernel, cfg),
        out_shape=(
            jax.ShapeDtypeStruct((R, S * W), F32),
            jax.ShapeDtypeStruct((R, QF), F32),
            jax.ShapeDtypeStruct((1, QF), F32),
        ),
        in_specs=[any_space] * 5 + [vmem] * 4,
        out_specs=(vmem, vmem, vmem),
        scratch_shapes=[
            pltpu.VMEM((T, QF), BF),
            pltpu.VMEM((T, S * W), BF),
            pltpu.VMEM((S, T, F), BF),
            pltpu.VMEM((S, T, F), BF),
            pltpu.VMEM((R, M), BF),
            pltpu.VMEM((R, QF), BF),
            pltpu.VMEM((folded + 16, (LH + UH) // fd), F32),
            pltpu.VMEM((D, 2, folded, (LH + UH) // fd), BF),
            pltpu.VMEM((D, 2, RP, LH + UH), BF),
            pltpu.VMEM((S, T, F), F32),
            pltpu.VMEM((T, D * RP), F32),
            pltpu.VMEM((T, LANES), F32),
            pltpu.VMEM((T, LANES), F32),
            pltpu.VMEM((T, hw), F32),
            pltpu.VMEM((T, hw), F32),
            pltpu.VMEM((ranks, T), BF),
            pltpu.VMEM((ranks, T), BF),
            pltpu.VMEM((S, small_rows, LANES), F32),
            pltpu.VMEM((S, small_rows, LANES), F32),
            pltpu.VMEM((small_rows, LANES), F32),
            pltpu.VMEM((D, small_rows, LANES), F32),
            pltpu.VMEM((small_rows, LANES), F32),
            pltpu.VMEM((S, small_rows, LANES), F32),
        ]
        + stage(F)
        + stage(W)
        + [dma((5,)), dma((S,)), dma((S,)), dma((D,)), dma((D,)), dma((D,)), dma((D,))]
        + [dma((S,)), dma((S,)), dma((D,)), dma((D,)), dma((S,)), dma((S,))]
        + [dma((2, K)), dma((2, K)), dma((2, K)), dma((2, K))]
        + [dma((2, D)), dma((2, D)), dma((2, S)), dma((2, S))],
        compiler_params=pltpu.CompilerParams(
            collective_id=0, has_side_effects=True, vmem_limit_bytes=56 * 1024 * 1024
        ),
    )(
        projections.reshape(T, QF),
        rotated_query_gradient.reshape(S, T, F),
        activations.reshape(T, M),
        adapter_lowering[0],
        adapter_raising[0],
        gains,
        jnp.asarray(lane_frequencies()),
        positions,
        valid.reshape(1, T),
    )
    down, up, gain = pl.pallas_call(
        place,
        out_shape=(
            jax.ShapeDtypeStruct((R, 1, M), F32),
            jax.ShapeDtypeStruct((R, 1, QF), F32),
            jax.ShapeDtypeStruct((1, QF), F32),
        ),
        in_specs=[vmem] * 3,
        out_specs=(vmem, vmem, vmem),
    )(down, up, gain)
    return down.reshape(1, R, M), up.reshape(1, R, QF), gain


def solution(mesh):
    in_specs = (
        P(None, "dp", "seq", None),
        P(None, "dp", None, "seq"),
        P(),
        P(None, "dp", None),
        P(None, "dp", None),
        P("dp", "seq", None),
        P(None, "dp", "seq"),
        P("dp", "seq"),
    )
    out_specs = (P(None, "dp", None), P(None, "dp", None), P())
    return jax.shard_map(shards, mesh=mesh, in_specs=in_specs, out_specs=out_specs, check_vma=False)
```

profile of v0, /device:TPU:0, one launch (start us, length us, event | category | flops | bytes accessed | tf_op | source)
XLA Modules:
  0.0 42.7 jit_solution(526949499685838983)
XLA Ops:
  0.6 40.2 %shard_map.112 = (f32[12,5120]{1,0:T(8,128)}, f32[12,4096]{1,0:T(8,128)}, f32[1,4096]{1,0:T(1,128)}) custom-call(bf16[128,4096]{1,0:T(8,128)(2,1)} %bitcast.8, bf16[8,128,512]{2,1,0:T(8,128)(2,1)} %bitcast.9, bf16[128,5120]{1,0:T(8,128)(2,1)} %bitcast.7, bf16[12,5120]{1,0:T(8,128)(2,1)} %bitcast.10, bf16[12,4096]{1,0:T(8,128)(2,1)} %bitcast.11, ...), custom_call_target="tpu_custom_call" | custom-call | tf_op jit(solution)/shard_map/pallas_call | solution.py:432
  40.9 1.9 %shard_map.113 = (f32[12,1,5120]{2,1,0:T(1,128)}, f32[12,1,4096]{2,1,0:T(1,128)}, f32[1,4096]{1,0:T(1,128)}) custom-call(f32[12,5120]{1,0:T(8,128)} %get-tuple-element.9.down_ref, f32[12,4096]{1,0:T(8,128)} %get-tuple-element.10.up_ref, f32[1,4096]{1,0:T(1,128)} %get-tuple-element.11.gain_ref), custom_call_target="tpu_custom_call" | custom-call | tf_op jit(solution)/shard_map/pallas_call | solution.py:486
where the time goes:
time: 42.9 us; the launch traced here: 42.7 us
  Pallas kernels  42.1 us (98%)
  between operations  0.64 us (1%)
    pallas_call x1, Pallas kernels, shards(): pl.pallas_call(functools.partial(kernel, cfg), out_shape=(jax.ShapeDtypeS...  40.2 us
    pallas_call x1, Pallas kernels, shards(): pl.pallas_call(place, out_shape=(jax.ShapeDtypeStruct((R, 1, M), F32), ja...  1.85 us

commit v1 on v0

v1 whole, which is shorter than its diff:
```python
import functools
from types import SimpleNamespace

import jax
import jax.numpy as jnp
import numpy as np
from jax import lax
from jax.experimental import pallas as pl
from jax.experimental.pallas import tpu as pltpu
from jax.sharding import PartitionSpec as P

HD = 128
EPSILON = 1e-06
LANES = 128
BF = jnp.bfloat16
F32 = jnp.float32
MESH = pl.DeviceIdType.MESH
NT = (((1,), (1,)), ((), ()))


def group_counts():
    one_sixth = HD // 6
    return (HD // 2 - 2 * one_sixth, one_sixth, one_sixth)


def lane_frequencies():
    pieces = []
    for n in group_counts():
        pieces.append(np.float32(10000.0) ** (-np.arange(n, dtype=np.float32) / np.float32(n)))
    return np.repeat(np.concatenate(pieces).astype(np.float32), 2)[None]


def kernel(cfg, tree, *refs):
    inputs, outputs, scratch = jax.tree.unflatten(tree, refs)
    m = SimpleNamespace(**inputs, **outputs, **scratch)
    S, D, T, F, W = cfg.S, cfg.D, cfg.T, cfg.F, cfg.W
    R, RP, M, QF, KD = cfg.R, cfg.RP, cfg.M, cfg.QF, cfg.KD
    pieces = cfg.pieces
    K = S // 2
    T2 = 2 * T
    ranks = D * R
    groups = F // LANES
    hw = 256 if F % 256 == 0 else 128
    pow2 = K & (K - 1) == 0
    d = lax.axis_index("dp")
    s = lax.axis_index("seq")
    c = lax.rem(s, 2)
    chip = s // 2
    sib = s + 1 - 2 * c

    def to(j):
        if j == 0:
            return chip
        if not pow2:
            return lax.rem(chip + j, K)
        k, bit = chip, 1
        while bit < K:
            if j & bit:
                k = k + bit * (1 - 2 * lax.rem(chip // bit, 2))
            bit *= 2
        return k

    def slot(j):
        return j if pow2 else (K - j) % K

    chips = [to(j) for j in range(K)]

    def frm(j):
        return chips[slot(j)]

    def cols(start, width):
        return pl.ds(pl.multiple_of(start, LANES), width)

    def rows(core):
        return pl.ds(pl.multiple_of(core * T, T), T)

    def copy(src, dst, ss, rs, dp, seq):
        return pltpu.make_async_remote_copy(
            src_ref=src, dst_ref=dst, send_sem=ss, recv_sem=rs,
            device_id=(dp, seq), device_id_type=MESH,
        )

    def other(cc):
        return c if cc == 0 else 1 - c

    peers = [(j, cc) for j in range(K) for cc in range(2) if (j, cc) != (0, 0)]

    barrier = pltpu.get_barrier_semaphore()
    for j, cc in peers:
        pl.semaphore_signal(barrier, inc=1, device_id=(d, 2 * chips[j] + other(cc)), device_id_type=MESH)
    for k in range(1, D):
        pl.semaphore_signal(barrier, inc=1, device_id=(lax.rem(d + k, D), s), device_id_type=MESH)

    def local(src, dst, i):
        return pltpu.make_async_copy(src, dst, m.local_sem.at[i])

    low_load = local(m.low_hbm, m.low, 0)
    rai_load = local(m.rai_hbm, m.rai, 1)
    pos_load = local(m.pos_hbm, m.pos.at[c], 2)
    valid_load = local(m.valid_hbm, m.valid.at[c], 3)
    freq_load = local(m.freq_hbm, m.freq, 4)
    gains_load = local(m.gains_hbm, m.gains, 5)
    cot_loads = [
        local(m.cot_hbm.at[chips[j]], m.cot.at[0] if j == 0 else m.cot_src.at[j - 1], 6 if j == 0 else 7)
        for j in range(K)
    ]
    proj_loads = [
        local(m.proj_hbm.at[:, cols((2 * k + c) * F, F)], m.p2.at[rows(c), pl.ds(k * F, F)], 8)
        for k in range(K)
    ]
    act_loads = [
        local(m.act_hbm.at[:, cols((2 * k + c) * W, W)], m.a2.at[rows(c), pl.ds(k * W, W)], 9)
        for k in range(KD)
    ]
    low_load.start()
    rai_load.start()
    for j in range(1, K):
        cot_loads[j].start()
    pos_load.start()
    valid_load.start()
    freq_load.start()
    gains_load.start()
    cot_loads[0].start()
    for load in proj_loads + act_loads:
        load.start()

    fold, packed = m.fold, m.packed
    if packed.shape[1] > K * R or KD < K:
        fold[...] = jnp.zeros_like(fold)
    if KD < K:
        m.a2[:, KD * W:] = jnp.zeros((T2, (K - KD) * W), BF)
    low_load.wait()
    rai_load.wait()
    for q in range(K):
        if q < KD:
            fold[q * R:(q + 1) * R, 0:W] = m.low[:, cols((2 * q + c) * W, W)].astype(F32)
        fold[q * R:(q + 1) * R, W:W + F] = m.rai[:, cols((2 * q + c) * F, F)].astype(F32)
    packed[d] = fold[...].astype(BF)
    local(m.cot_hbm.at[0:K - 1], m.cot_src, 7).wait()

    def cot_copy(j, r):
        part = pl.ds(r * T, T)
        return copy(m.cot_src.at[j - 1, part], m.cot.at[j, part],
                    m.cot_s, m.cot_r.at[j, r], d, 2 * chips[j] + c)

    def adapt_copy(peer, place):
        return copy(packed.at[place], packed.at[place], m.ad_s, m.ad_r, peer, s)

    def sib_copy(src, dst, i):
        return copy(src, dst, m.sib_s.at[i], m.sib_r.at[i], d, sib)

    def pos_copy(core):
        return sib_copy(m.pos_hbm, m.pos.at[core], 0)

    def valid_copy(core):
        return sib_copy(m.valid_hbm, m.valid.at[core], 1)

    def proj_copy(k, core):
        return sib_copy(m.proj_hbm.at[:, cols((2 * k + 1 - c) * F, F)],
                        m.p2.at[rows(core), pl.ds(k * F, F)], 6)

    def act_copy(k, core):
        return sib_copy(m.act_hbm.at[:, cols((2 * k + 1 - c) * W, W)],
                        m.a2.at[rows(core), pl.ds(k * W, W)], 7)

    def xch_copy(send, recv, i):
        return sib_copy(send, recv, i)

    sq_copy = xch_copy(m.sq_send, m.sq_recv, 2)
    red_copy = xch_copy(m.red_send, m.red_recv, 3)
    dot_copy = xch_copy(m.dot_send, m.dot_recv, 4)
    back_copy = xch_copy(m.back_send, m.back_recv, 5)

    near = [j for j in range(1, K) if pow2 and j & (j - 1) == 0]
    far = [j for j in range(1, K) if j not in near]
    order = [(j, r) for r in range(2) for j in near] + [(j, r) for j in far for r in range(2)]

    pl.semaphore_wait(barrier, S + D - 2)
    for j, r in order:
        cot_copy(j, r).start()
    for k in range(1, D):
        adapt_copy(lax.rem(d + k, D), d).start()
    pos_copy(c).start()
    valid_copy(c).start()
    for k in range(K):
        proj_copy(k, c).start()
    for k in range(KD):
        act_copy(k, c).start()

    row_i = lax.broadcasted_iota(jnp.int32, (hw, hw), 0)
    col_i = lax.broadcasted_iota(jnp.int32, (hw, hw), 1)
    even = lax.rem(col_i, 2) == 0
    m.swap[...] = jnp.where(
        even & (row_i == col_i + 1), 1.0, jnp.where(jnp.logical_not(even) & (row_i == col_i - 1), -1.0, 0.0)
    ).astype(BF)

    pos_load.wait()
    valid_load.wait()
    freq_load.wait()
    gains_load.wait()
    pos_copy(1 - c).wait_recv()
    valid_copy(1 - c).wait_recv()
    n0, n1, _ = group_counts()
    lane = lax.broadcasted_iota(jnp.int32, (T, LANES), 1)

    def column(row):
        return jnp.broadcast_to(row.astype(F32), (LANES, T)).T

    count = jnp.zeros((1, 1), F32)
    for h in range(2):
        index = jnp.where(
            lane < 2 * n0, column(m.pos[h, 0]),
            jnp.where(lane < 2 * (n0 + n1), column(m.pos[h, 1]), column(m.pos[h, 2])),
        )
        angle = index * m.freq[...]
        ok = column(m.valid[h])
        m.cos[h * T:(h + 1) * T, :] = jnp.cos(angle) * ok
        m.sin[h * T:(h + 1) * T, :] = jnp.sin(angle) * ok
        count += jnp.sum(m.valid[h].astype(F32), axis=1, keepdims=True)
    m.small_send[...] = jnp.broadcast_to(count[:, :, None], m.small_send.shape)

    proj_all = m.proj_hbm.at[:, 0:K * F]
    local(proj_all, m.p2.at[rows(c)], 8).wait()
    sib_proj = sib_copy(proj_all, m.p2.at[rows(1 - c)], 6)
    sib_proj.wait_recv()
    square = jnp.zeros((T2, LANES), F32)
    for i in range(K * groups):
        v = m.p2[:, i * LANES:(i + 1) * LANES].astype(F32)
        square += v * v
    m.sq_send[...] = square
    sq_copy.start()
    m.dot_send[...] = jnp.zeros_like(m.dot_send)
    cot_loads[0].wait()
    sq_copy.wait_recv()
    square = m.sq_send[...] + m.sq_recv[...]
    inverse = lax.rsqrt(jnp.sum(square, axis=1, keepdims=True) / QF + EPSILON)
    m.inv[...] = jnp.broadcast_to(inverse, (T2, LANES))

    def wide(x):
        return jnp.concatenate([x] * (hw // LANES), axis=1) if hw > LANES else x

    def chunk(j, r):
        k = frm(j)
        part = slice(r * T, (r + 1) * T)
        inv = wide(m.inv[part])
        cw, sw = wide(m.cos[part]), wide(m.sin[part])
        for i in range(F // hw):
            x = m.cot[j, part, i * hw:(i + 1) * hw]
            xs = jnp.dot(x, m.swap[...], preferred_element_type=F32)
            un = cw * x.astype(F32) + sw * xs
            prod = un * (m.p2[part, cols(k * F + i * hw, hw)].astype(F32) * inv)
            g = jnp.sum(prod, axis=0, keepdims=True)
            for t in range(hw // LANES):
                n = i * (hw // LANES) + t
                piece = g[:, t * LANES:(t + 1) * LANES]
                if r > 0:
                    piece += m.small_send[j, n:n + 1, :]
                m.small_send[j, n:n + 1, :] = piece
            gn = m.gains[:, cols((2 * k + c) * F + i * hw, hw)]
            m.scaled[j, part, i * hw:(i + 1) * hw] = un * gn
            pg = prod * gn
            acc = pg[:, :LANES]
            for t in range(1, hw // LANES):
                acc += pg[:, t * LANES:(t + 1) * LANES]
            m.dot_send[part] += acc

    chunk(0, 0)
    chunk(0, 1)
    cut = len(order) - 1
    for j, r in order[:cut]:
        cot_copy(j, r).wait_recv()
        chunk(j, r)

    adapt_all = copy(packed.at[0:D - 1], packed.at[0:D - 1], m.ad_s, m.ad_r, d, sib)
    adapt_all.wait_recv()
    adaptf, adapt = m.adaptf, m.adapt
    for e in range(D):
        fold[...] = packed[e].astype(F32)
        for q in range(K):
            adaptf[q, e * R:(e + 1) * R, :] = fold[q * R:(q + 1) * R, :]
    for q in range(K):
        adapt[q] = adaptf[q].astype(BF)
    act_all = m.act_hbm.at[:, 0:KD * W]
    local(act_all, m.a2.at[rows(c), 0:KD * W], 9).wait()
    sib_act = sib_copy(act_all, m.a2.at[rows(1 - c), 0:KD * W], 7)
    sib_act.wait_recv()
    red = jnp.zeros((ranks, T2), F32)
    for k in range(KD):
        red += lax.dot_general(adapt[k, :, 0:W], m.a2[:, k * W:(k + 1) * W], NT, preferred_element_type=F32)
    m.red_send[...] = red
    red_copy.start()

    for j, r in order[cut:]:
        cot_copy(j, r).wait_recv()
        chunk(j, r)

    dot_copy.start()

    def small_copy(j):
        return copy(m.small_send.at[slot(j)], m.small_recv.at[j - 1], m.sm_s, m.sm_r, d, 2 * chips[j] + c)

    for j in range(1, K):
        small_copy(j).start()
    red_copy.wait_recv()
    redt = (m.red_send[...] + m.red_recv[...]).astype(BF)
    m.redt[...] = redt
    dot_copy.wait_recv()
    mean = jnp.sum(m.dot_send[...] + m.dot_recv[...], axis=1, keepdims=True) / QF
    inv = m.inv[...]
    m.coef[...] = inv * inv * jnp.broadcast_to(mean, (T2, LANES))

    def rs_copy(i, j):
        return copy(m.rs_send[i].at[j - 1], m.rs_recv[i].at[j - 1],
                    m.rs_s.at[i], m.rs_r.at[i], d, 2 * chips[j] + c)

    def whole(src, dst, ss, rs):
        return copy(src, dst, ss, rs, d, sib)

    back = jnp.zeros((ranks, T2), F32)
    for js in (near, far + [0]):
        for j in js:
            k = chips[j]
            inv, coef = wide(m.inv[...]), wide(m.coef[...])
            for i in range(F // hw):
                part = slice(i * hw, (i + 1) * hw)
                p = m.p2[:, cols(k * F + i * hw, hw)].astype(F32)
                delta = (inv * m.scaled[slot(j), :, part] - coef * p).astype(BF)
                raising = adapt[k, :, W + i * hw:W + (i + 1) * hw]
                back += lax.dot_general(raising, delta, NT, preferred_element_type=F32)
                term = jnp.dot(m.redt[...], delta, preferred_element_type=F32)
                if j == 0:
                    m.own[0][:, part] = term
                else:
                    m.rs_send[0][j - 1, :, part] = term.astype(BF)
        for j in js:
            if j > 0:
                rs_copy(0, j).start()
    m.back_send[...] = back
    back_copy.start()
    back_copy.wait_recv()
    m.backt[...] = (m.back_send[...] + m.back_recv[...]).astype(BF)

    for i, (kind, off, width) in enumerate(pieces):
        if kind == "u":
            continue
        for j in list(range(1, K)) + [0]:
            term = jnp.dot(m.backt[...], m.a2[:, cols(chips[j] * W + off, width)], preferred_element_type=F32)
            if j == 0:
                m.own[i][...] = term
            else:
                m.rs_send[i][j - 1] = term.astype(BF)
        for j in range(1, K):
            rs_copy(i, j).start()

    small = m.small_send[0]
    small_all = whole(m.small_recv, m.small_recv, m.sm_s, m.sm_r)
    small_all.wait_recv()
    for j in range(1, K):
        small += m.small_recv[j - 1]
    m.small_dp[...] = small

    def small_dp_copy(k):
        return copy(m.small_dp, m.small_dp_recv.at[k - 1], m.smd_s, m.smd_r, lax.rem(d + k, D), s)

    for k in range(1, D):
        small_dp_copy(k).start()

    def dp_copy(i, k):
        return copy(m.dp_send[i].at[lax.rem(d + k, D)], m.dp_recv[i].at[k - 1],
                    m.dp_s.at[i], m.dp_r.at[i], lax.rem(d + k, D), s)

    def dp_stage(i):
        total = m.own[i][...]
        whole(m.rs_send[i], m.rs_recv[i], m.rs_s.at[i], m.rs_r.at[i]).wait_recv()
        for j in range(1, K):
            total += m.rs_recv[i][j - 1].astype(F32)
        tot = m.tot[i]
        tot[0:ranks, :] = total
        for e in range(D):
            block = tot[e * R:e * R + RP, :]
            m.dp_f[i][e] = block
            m.dp_send[i][e] = block.astype(BF)
        for k in range(1, D):
            dp_copy(i, k).start()

    def ag_copy(i, j, cc):
        return copy(m.fin[i], m.ag[i].at[2 * j + cc - 1], m.ag_s.at[i], m.ag_r.at[i],
                    d, 2 * chips[j] + other(cc))

    def put(i, q, value):
        kind, off, width = pieces[i]
        out, base = (m.up_out, q * F) if kind == "u" else (m.down_out, q * W + off)

        def store():
            where = cols(base, width)
            for r in range(R):
                out[r, :, where] = value[r:r + 1]

        if kind == "d" and S * W != M:
            pl.when(base + width <= M)(store)
        else:
            store()

    def dp_all(i):
        return whole(m.dp_send[i].at[0:D - 1], m.dp_recv[i], m.dp_s.at[i], m.dp_r.at[i])

    def ag_all(i):
        return whole(m.ag[i], m.ag[i], m.ag_s.at[i], m.ag_r.at[i])

    def gather(i, factor):
        total = m.dp_f[i][d]
        dp_all(i).wait_recv()
        for k in range(1, D):
            total += m.dp_recv[i][k - 1].astype(F32)
        fin = (total * factor).astype(BF)
        m.fin[i][...] = fin
        for j, cc in peers:
            ag_copy(i, j, cc).start()
        put(i, s, fin.astype(F32))

    for i in range(len(pieces)):
        dp_stage(i)

    small = m.small_dp[...]
    small_dp_all = whole(m.small_dp_recv, m.small_dp_recv, m.smd_s, m.smd_r)
    small_dp_all.wait_recv()
    for k in range(1, D):
        small += m.small_dp_recv[k - 1]
    factor = F32(cfg.tokens) / small[groups:groups + 1, 0:1]
    m.small_fin[...] = small * factor

    def small_ag_copy(j, cc):
        return copy(m.small_fin, m.small_ag.at[2 * j + cc - 1], m.sma_s, m.sma_r,
                    d, 2 * chips[j] + other(cc))

    for j, cc in peers:
        small_ag_copy(j, cc).start()

    for i in range(len(pieces)):
        gather(i, factor)

    def put_gain(q, value):
        for n in range(groups):
            m.gain_out[:, cols(q * F + n * LANES, LANES)] = value[n:n + 1, :]

    put_gain(s, m.small_fin[...])
    small_ag_all = whole(m.small_ag, m.small_ag, m.sma_s, m.sma_r)
    small_ag_all.wait_recv()
    for j, cc in peers:
        put_gain(2 * frm(j) + other(cc), m.small_ag[2 * j + cc - 1])
    for i in range(len(pieces)):
        ag_all(i).wait_recv()
        for j, cc in peers:
            put(i, 2 * frm(j) + other(cc), m.ag[i][2 * j + cc - 1].astype(F32))

    pos_copy(c).wait_send()
    valid_copy(c).wait_send()
    whole(m.cot_src, m.cot_src, m.cot_s, m.cot_r.at[0, 0]).wait_send()
    for group in (sib_proj, sib_act, sq_copy, red_copy, dot_copy, back_copy,
                  adapt_all, small_all, small_dp_all, small_ag_all):
        group.wait_send()
    for i in range(len(pieces)):
        whole(m.rs_send[i], m.rs_recv[i], m.rs_s.at[i], m.rs_r.at[i]).wait_send()
        dp_all(i).wait_send()
        ag_all(i).wait_send()


def write_out(*refs):
    n = len(refs) // 2
    copies = [pltpu.make_async_copy(refs[i], refs[n + i], refs[2 * n].at[i]) for i in range(n)]
    for copy in copies:
        copy.start()
    for copy in copies:
        copy.wait()


def block_width(M, S):
    width = -(-M // (LANES * S)) * LANES
    while M % (2 * width):
        width += LANES
    return width


def shards(projections, rotated_query_gradient, gains, adapter_lowering, adapter_raising,
           activations, positions, valid):
    D, S = lax.axis_size("dp"), lax.axis_size("seq")
    T, QF = projections.shape[2:]
    F = rotated_query_gradient.shape[3]
    R, M = adapter_lowering.shape[1:]
    W = block_width(M, S)
    KD = M // (2 * W)
    RP = -(-R // 16) * 16
    K = S // 2
    T2 = 2 * T
    ranks = D * R
    folded = -(-K * R // 16) * 16
    first = -(-W // (2 * LANES)) * LANES
    pieces = [("u", 0, F), ("d", 0, first)] + ([("d", first, W - first)] if W > first else [])
    cfg = SimpleNamespace(S=S, D=D, T=T, F=F, W=W, R=R, RP=RP, M=M, QF=QF, KD=KD, tokens=D * S * T, pieces=pieces)

    hw = 256 if F % 256 == 0 else 128
    small_rows = -(-(F // LANES + 1) // 8) * 8
    vmem = pltpu.VMEM
    dma = pltpu.SemaphoreType.DMA
    scratch = dict(
        p2=vmem((T2, K * F), BF),
        a2=vmem((T2, K * W), BF),
        cot=vmem((K, T2, F), BF),
        cot_src=vmem((K - 1, T2, F), BF),
        low=vmem((R, M), BF),
        rai=vmem((R, QF), BF),
        pos=vmem((2, 3, 1, T), jnp.int32),
        valid=vmem((2, 1, T), jnp.int32),
        freq=vmem((1, LANES), F32),
        gains=vmem((1, QF), F32),
        swap=vmem((hw, hw), BF),
        fold=vmem((folded, W + F), F32),
        packed=vmem((D, folded, W + F), BF),
        adaptf=vmem((K, ranks, W + F), F32),
        adapt=vmem((K, ranks, W + F), BF),
        scaled=vmem((K, T2, F), F32),
        cos=vmem((T2, LANES), F32),
        sin=vmem((T2, LANES), F32),
        inv=vmem((T2, LANES), F32),
        coef=vmem((T2, LANES), F32),
        sq_send=vmem((T2, LANES), F32),
        sq_recv=vmem((T2, LANES), F32),
        dot_send=vmem((T2, LANES), F32),
        dot_recv=vmem((T2, LANES), F32),
        red_send=vmem((ranks, T2), F32),
        red_recv=vmem((ranks, T2), F32),
        back_send=vmem((ranks, T2), F32),
        back_recv=vmem((ranks, T2), F32),
        redt=vmem((ranks, T2), BF),
        backt=vmem((ranks, T2), BF),
        small_send=vmem((K, small_rows, LANES), F32),
        small_recv=vmem((K - 1, small_rows, LANES), F32),
        small_dp=vmem((small_rows, LANES), F32),
        small_dp_recv=vmem((D - 1, small_rows, LANES), F32),
        small_fin=vmem((small_rows, LANES), F32),
        small_ag=vmem((S - 1, small_rows, LANES), F32),
    )
    for kind, off, width in pieces:
        for name, value in dict(
            rs_send=vmem((K - 1, ranks, width), BF),
            rs_recv=vmem((K - 1, ranks, width), BF),
            own=vmem((ranks, width), F32),
            tot=vmem((ranks + RP, width), F32),
            dp_f=vmem((D, RP, width), F32),
            dp_send=vmem((D, RP, width), BF),
            dp_recv=vmem((D - 1, RP, width), BF),
            fin=vmem((RP, width), BF),
            ag=vmem((S - 1, RP, width), BF),
        ).items():
            scratch.setdefault(name, []).append(value)
    n = len(pieces)
    sems = dict(
        local_sem=(10,), cot_s=(), cot_r=(K, 2), ad_s=(), ad_r=(), sib_s=(8,), sib_r=(8,),
        sm_s=(), sm_r=(), smd_s=(), smd_r=(), sma_s=(), sma_r=(),
        rs_s=(n,), rs_r=(n,), dp_s=(n,), dp_r=(n,), ag_s=(n,), ag_r=(n,),
    )
    scratch.update({name: dma(shape) if shape else dma for name, shape in sems.items()})
    hbm = pl.BlockSpec(memory_space=pltpu.HBM)
    inputs = dict(
        proj_hbm=projections.reshape(T, QF),
        cot_hbm=rotated_query_gradient.reshape(K, T2, F),
        act_hbm=activations.reshape(T, M),
        low_hbm=adapter_lowering[0],
        rai_hbm=adapter_raising[0],
        gains_hbm=gains,
        freq_hbm=jnp.asarray(lane_frequencies()),
        pos_hbm=positions,
        valid_hbm=valid.reshape(1, T),
    )
    outputs = dict(
        down_out=jax.ShapeDtypeStruct((R, 1, M), F32),
        up_out=jax.ShapeDtypeStruct((R, 1, QF), F32),
        gain_out=jax.ShapeDtypeStruct((1, QF), F32),
    )
    leaves, tree = jax.tree.flatten([inputs, outputs, scratch])
    count = len(inputs) + len(outputs)
    results = pl.pallas_call(
        functools.partial(kernel, cfg, tree),
        out_shape=leaves[len(inputs):count],
        in_specs=[hbm] * len(inputs),
        out_specs=[pl.BlockSpec(memory_space=vmem)] * len(outputs),
        scratch_shapes=leaves[count:],
        compiler_params=pltpu.CompilerParams(
            collective_id=0, has_side_effects=True, vmem_limit_bytes=40 * 1024 * 1024
        ),
    )(*[pltpu.with_memory_space_constraint(x, pltpu.HBM) for x in leaves[:len(inputs)]])
    results = pl.pallas_call(
        write_out,
        out_shape=leaves[len(inputs):count],
        in_specs=[pl.BlockSpec(memory_space=vmem)] * len(outputs),
        out_specs=[hbm] * len(outputs),
        scratch_shapes=[dma((len(outputs),))],
        compiler_params=pltpu.CompilerParams(vmem_limit_bytes=1024 * 1024),
    )(*results)
    down, gain, up = results
    return down.reshape(1, R, M), up.reshape(1, R, QF), gain


def solution(mesh):
    in_specs = (
        P(None, "dp", "seq", None),
        P(None, "dp", None, "seq"),
        P(),
        P(None, "dp", None),
        P(None, "dp", None),
        P("dp", "seq", None),
        P(None, "dp", "seq"),
        P("dp", "seq"),
    )
    out_specs = (P(None, "dp", None), P(None, "dp", None), P())
    return jax.shard_map(shards, mesh=mesh, in_specs=in_specs, out_specs=out_specs, check_vma=False)
```

time: 42.9 us -> 36.8 us (0.86)
  Pallas kernels: 42.1 us -> 36 us
    pallas_call x2, Pallas kernels: 42.1 us -> 36 us  [the longest x1 35.2 us: shards(): pl.pallas_call(functools.partial(kernel, cfg, tree), out_shape=leaves[len...]
where the time goes in v1:
time: 36.8 us; the launch traced here: 36.6 us
  Pallas kernels  36 us (98%)
  between operations  0.64 us (2%)
    pallas_call x1, Pallas kernels, shards(): pl.pallas_call(functools.partial(kernel, cfg, tree), out_shape=leaves[len...  35.2 us
    pallas_call x1, Pallas kernels, shards(): pl.pallas_call(write_out, out_shape=leaves[len(inputs):count], in_specs=[...  0.79 us

profile of v1, /device:TPU:0, one launch (start us, length us, event | category | flops | bytes accessed | tf_op | source)
XLA Modules:
  0.0 36.6 jit_solution(6580407487114755261)
XLA Ops:
  0.6 35.2 %shard_map.112 = (f32[12,1,5120]{2,1,0:T(1,128)S(1)}, f32[1,4096]{1,0:T(1,128)S(1)}, f32[12,1,4096]{2,1,0:T(1,128)S(1)}) custom-call(bf16[128,5120]{1,0:T(8,128)(2,1)} %bitcast.7, bf16[4,256,512]{2,1,0:T(8,128)(2,1)} %bitcast.8, f32[1,128]{1,0:T(1,128)} %constant.2.clone.refs_2_, f32[1,4096]{1,0:T(1,128)} %refs_3_.1, bf16[12,5120]{1,0:T(8,128)(2,1)} %bitcast.10, ...), custom_call_target="tpu_custom_call" | custom-call | tf_op jit(solution)/shard_map/pallas_call | solution.py:582
  35.8 0.8 %shard_map.113 = (f32[12,1,5120]{2,1,0:T(1,128)}, f32[1,4096]{1,0:T(1,128)}, f32[12,1,4096]{2,1,0:T(1,128)}) custom-call(f32[12,1,5120]{2,1,0:T(1,128)S(1)} %get-tuple-element.9.refs_0_, f32[1,4096]{1,0:T(1,128)S(1)} %get-tuple-element.10.refs_1_, f32[12,1,4096]{2,1,0:T(1,128)S(1)} %get-tuple-element.11.refs_2_), custom_call_target="tpu_custom_call" | custom-call | tf_op jit(solution)/shard_map/pallas_call | solution.py:592

commit v2 on v1

--- a/solution.py
+++ b/solution.py
@@ -34,7 +34,7 @@
     inputs, outputs, scratch = jax.tree.unflatten(tree, refs)
     m = SimpleNamespace(**inputs, **outputs, **scratch)
     S, D, T, F, W = cfg.S, cfg.D, cfg.T, cfg.F, cfg.W
-    R, RP, M, QF, KD = cfg.R, cfg.RP, cfg.M, cfg.QF, cfg.KD
+    R, RP, M, QF, KD, Z = cfg.R, cfg.RP, cfg.M, cfg.QF, cfg.KD, cfg.Z
     pieces = cfg.pieces
     K = S // 2
     T2 = 2 * T
@@ -101,7 +101,7 @@
     freq_load = local(m.freq_hbm, m.freq, 4)
     gains_load = local(m.gains_hbm, m.gains, 5)
     cot_loads = [
-        local(m.cot_hbm.at[chips[j]], m.cot.at[0] if j == 0 else m.cot_src.at[j - 1], 6 if j == 0 else 7)
+        local(m.cot_hbm.at[chips[j]], m.cot.at[0] if j == 0 else m.cot_src.at[j - 1], 10 + j)
         for j in range(K)
     ]
     proj_loads = [
@@ -112,10 +112,10 @@
         local(m.act_hbm.at[:, cols((2 * k + c) * W, W)], m.a2.at[rows(c), pl.ds(k * W, W)], 9)
         for k in range(KD)
     ]
+    for j in range(1, K):
+        cot_loads[j].start()
     low_load.start()
     rai_load.start()
-    for j in range(1, K):
-        cot_loads[j].start()
     pos_load.start()
     valid_load.start()
     freq_load.start()
@@ -124,8 +124,65 @@
     for load in proj_loads + act_loads:
         load.start()
 
-    fold, packed = m.fold, m.packed
-    if packed.shape[1] > K * R or KD < K:
+    def cot_copy(j, r):
+        part = pl.ds(r * T, T)
+        return copy(m.cot_src.at[j - 1, part], m.cot.at[j, part],
+                    m.cot_s, m.cot_r.at[j, r], d, 2 * chips[j] + c)
+
+    def raise_copy(k):
+        return copy(m.packed_r.at[d], m.packed_r.at[d], m.ar_s, m.ar_r, lax.rem(d + k, D), s)
+
+    def lower_copy(k):
+        return copy(m.packed_l.at[d], m.packed_l.at[d], m.al_s, m.al_r, lax.rem(d + k, D), s)
+
+    def sib_copy(src, dst, i):
+        return copy(src, dst, m.sib_s.at[i], m.sib_r.at[i], d, sib)
+
+    def pos_copy(core):
+        return sib_copy(m.pos_hbm, m.pos.at[core], 0)
+
+    def valid_copy(core):
+        return sib_copy(m.valid_hbm, m.valid.at[core], 1)
+
+    def proj_copy(k, core):
+        return sib_copy(m.proj_hbm.at[:, cols((2 * k + 1 - c) * F, F)],
+                        m.p2.at[rows(core), pl.ds(k * F, F)], 6)
+
+    def act_copy(k, core):
+        return sib_copy(m.act_hbm.at[:, cols((2 * k + 1 - c) * W, W)],
+                        m.a2.at[rows(core), pl.ds(k * W, W)], 7)
+
+    def xch_copy(send, recv, i):
+        return sib_copy(send, recv, i)
+
+    sq_copy = xch_copy(m.sq_send, m.sq_recv, 2)
+    red_copy = xch_copy(m.red_send, m.red_recv, 3)
+    base_copy = xch_copy(m.base_send, m.base_recv, 4)
+    back_copy = xch_copy(m.back_send, m.back_recv, 5)
+
+    near = [j for j in range(1, K) if pow2 and j & (j - 1) == 0]
+    far = [j for j in range(1, K) if j not in near]
+    order = [(j, r) for r in range(2) for j in near] + [(j, r) for j in far for r in range(2)]
+
+    pl.semaphore_wait(barrier, S + D - 2)
+    pos_copy(c).start()
+    valid_copy(c).start()
+    for j in near:
+        cot_loads[j].wait()
+        cot_copy(j, 0).start()
+    for j in near:
+        cot_copy(j, 1).start()
+    for j in far:
+        cot_loads[j].wait()
+
+    def far_sends():
+        for j in far:
+            for r in range(2):
+                cot_copy(j, r).start()
+
+    pl.when(c == 0)(far_sends)
+    fold = m.fold
+    if fold.shape[0] > K * R or KD < K:
         fold[...] = jnp.zeros_like(fold)
     if KD < K:
         m.a2[:, KD * W:] = jnp.zeros((T2, (K - KD) * W), BF)
@@ -135,53 +192,13 @@
         if q < KD:
             fold[q * R:(q + 1) * R, 0:W] = m.low[:, cols((2 * q + c) * W, W)].astype(F32)
         fold[q * R:(q + 1) * R, W:W + F] = m.rai[:, cols((2 * q + c) * F, F)].astype(F32)
-    packed[d] = fold[...].astype(BF)
-    local(m.cot_hbm.at[0:K - 1], m.cot_src, 7).wait()
-
-    def cot_copy(j, r):
-        part = pl.ds(r * T, T)
-        return copy(m.cot_src.at[j - 1, part], m.cot.at[j, part],
-                    m.cot_s, m.cot_r.at[j, r], d, 2 * chips[j] + c)
-
-    def adapt_copy(peer, place):
-        return copy(packed.at[place], packed.at[place], m.ad_s, m.ad_r, peer, s)
-
-    def sib_copy(src, dst, i):
-        return copy(src, dst, m.sib_s.at[i], m.sib_r.at[i], d, sib)
-
-    def pos_copy(core):
-        return sib_copy(m.pos_hbm, m.pos.at[core], 0)
-
-    def valid_copy(core):
-        return sib_copy(m.valid_hbm, m.valid.at[core], 1)
-
-    def proj_copy(k, core):
-        return sib_copy(m.proj_hbm.at[:, cols((2 * k + 1 - c) * F, F)],
-                        m.p2.at[rows(core), pl.ds(k * F, F)], 6)
-
-    def act_copy(k, core):
-        return sib_copy(m.act_hbm.at[:, cols((2 * k + 1 - c) * W, W)],
-                        m.a2.at[rows(core), pl.ds(k * W, W)], 7)
-
-    def xch_copy(send, recv, i):
-        return sib_copy(send, recv, i)
-
-    sq_copy = xch_copy(m.sq_send, m.sq_recv, 2)
-    red_copy = xch_copy(m.red_send, m.red_recv, 3)
-    dot_copy = xch_copy(m.dot_send, m.dot_recv, 4)
-    back_copy = xch_copy(m.back_send, m.back_recv, 5)
-
-    near = [j for j in range(1, K) if pow2 and j & (j - 1) == 0]
-    far = [j for j in range(1, K) if j not in near]
-    order = [(j, r) for r in range(2) for j in near] + [(j, r) for j in far for r in range(2)]
-
-    pl.semaphore_wait(barrier, S + D - 2)
-    for j, r in order:
-        cot_copy(j, r).start()
+    m.packed_r[d] = fold[:, W:].astype(BF)
+    m.packed_l[d] = fold[:, :W].astype(BF)
+
     for k in range(1, D):
-        adapt_copy(lax.rem(d + k, D), d).start()
-    pos_copy(c).start()
-    valid_copy(c).start()
+        raise_copy(k).start()
+    for k in range(1, D):
+        lower_copy(k).start()
     for k in range(K):
         proj_copy(k, c).start()
     for k in range(KD):
@@ -229,12 +246,14 @@
         square += v * v
     m.sq_send[...] = square
     sq_copy.start()
-    m.dot_send[...] = jnp.zeros_like(m.dot_send)
+    m.dot[...] = jnp.zeros_like(m.dot)
     cot_loads[0].wait()
     sq_copy.wait_recv()
     square = m.sq_send[...] + m.sq_recv[...]
     inverse = lax.rsqrt(jnp.sum(square, axis=1, keepdims=True) / QF + EPSILON)
-    m.inv[...] = jnp.broadcast_to(inverse, (T2, LANES))
+    inverse = jnp.broadcast_to(inverse, (T2, LANES))
+    m.inv[...] = inverse
+    m.inv_row[...] = inverse.T[0:1, :]
 
     def wide(x):
         return jnp.concatenate([x] * (hw // LANES), axis=1) if hw > LANES else x
@@ -257,44 +276,82 @@
                     piece += m.small_send[j, n:n + 1, :]
                 m.small_send[j, n:n + 1, :] = piece
             gn = m.gains[:, cols((2 * k + c) * F + i * hw, hw)]
-            m.scaled[j, part, i * hw:(i + 1) * hw] = un * gn
+            m.scaled[j, part, i * hw:(i + 1) * hw] = un * gn * inv
             pg = prod * gn
             acc = pg[:, :LANES]
             for t in range(1, hw // LANES):
                 acc += pg[:, t * LANES:(t + 1) * LANES]
-            m.dot_send[part] += acc
+            m.dot[part] += acc
+
+    def whole(src, dst, ss, rs):
+        return copy(src, dst, ss, rs, d, sib)
+
+    def unfold(packed, adaptf, adapt):
+        for e in range(D):
+            fold[:, :packed.shape[2]] = packed[e].astype(F32)
+            for q in range(K):
+                adaptf[q, e * R:(e + 1) * R, :] = fold[q * R:(q + 1) * R, :packed.shape[2]]
+        for q in range(K):
+            adapt[q] = adaptf[q].astype(BF)
+
+    def back_part(j, r):
+        part = slice(r * T, (r + 1) * T)
+        raising = m.adapt_r[frm(j)]
+        value = m.scaled[j, part, :]
+        high = value.astype(BF)
+        low = (value - high.astype(F32)).astype(BF)
+        term = lax.dot_general(raising, high, NT, preferred_element_type=F32)
+        return term + lax.dot_general(raising, low, NT, preferred_element_type=F32)
 
     chunk(0, 0)
     chunk(0, 1)
-    cut = len(order) - 1
-    for j, r in order[:cut]:
+    split = 2 * len(near)
+    for (j, r), n in zip(order[:split], range(split)):
+        cot_copy(j, r).wait_recv()
+        if n == 2:
+            pl.when(c == 1)(far_sends)
+        chunk(j, r)
+    raise_all = whole(m.packed_r.at[0:D - 1], m.packed_r.at[0:D - 1], m.ar_s, m.ar_r)
+    raise_all.wait_recv()
+    unfold(m.packed_r, m.adaptf_r, m.adapt_r)
+    base = jnp.zeros((ranks, T2), F32)
+    for k in range(K):
+        base += lax.dot_general(m.adapt_r[k], m.p2[:, k * F:(k + 1) * F], NT, preferred_element_type=F32)
+    m.base_send[...] = base
+    base_copy.start()
+    for r in range(2):
+        total = jnp.zeros((ranks, T), F32)
+        for j in [0] + near:
+            total += back_part(j, r)
+        m.back_send[0:ranks, r * T:(r + 1) * T] = total
+
+    for j, r in order[split:-1]:
         cot_copy(j, r).wait_recv()
         chunk(j, r)
-
-    adapt_all = copy(packed.at[0:D - 1], packed.at[0:D - 1], m.ad_s, m.ad_r, d, sib)
-    adapt_all.wait_recv()
-    adaptf, adapt = m.adaptf, m.adapt
-    for e in range(D):
-        fold[...] = packed[e].astype(F32)
-        for q in range(K):
-            adaptf[q, e * R:(e + 1) * R, :] = fold[q * R:(q + 1) * R, :]
-    for q in range(K):
-        adapt[q] = adaptf[q].astype(BF)
+        m.back_send[0:ranks, r * T:(r + 1) * T] += back_part(j, r)
+    lower_all = whole(m.packed_l.at[0:D - 1], m.packed_l.at[0:D - 1], m.al_s, m.al_r)
+    lower_all.wait_recv()
+    unfold(m.packed_l, m.adaptf_l, m.adapt_l)
     act_all = m.act_hbm.at[:, 0:KD * W]
     local(act_all, m.a2.at[rows(c), 0:KD * W], 9).wait()
     sib_act = sib_copy(act_all, m.a2.at[rows(1 - c), 0:KD * W], 7)
     sib_act.wait_recv()
     red = jnp.zeros((ranks, T2), F32)
     for k in range(KD):
-        red += lax.dot_general(adapt[k, :, 0:W], m.a2[:, k * W:(k + 1) * W], NT, preferred_element_type=F32)
+        red += lax.dot_general(m.adapt_l[k], m.a2[:, k * W:(k + 1) * W], NT, preferred_element_type=F32)
     m.red_send[...] = red
     red_copy.start()
-
-    for j, r in order[cut:]:
+    base_copy.wait_recv()
+    inv_row = m.inv_row[...]
+    m.base[...] = (m.base_send[...] + m.base_recv[...]) * (inv_row * inv_row)
+
+    for j, r in order[-1:]:
         cot_copy(j, r).wait_recv()
         chunk(j, r)
-
-    dot_copy.start()
+        m.back_send[0:ranks, r * T:(r + 1) * T] += back_part(j, r)
+    dot_row = jnp.sum(m.dot[...].T, axis=0, keepdims=True)
+    m.back_send[ranks:ranks + 8, :] = jnp.broadcast_to(dot_row, (8, T2))
+    back_copy.start()
 
     def small_copy(j):
         return copy(m.small_send.at[slot(j)], m.small_recv.at[j - 1], m.sm_s, m.sm_r, d, 2 * chips[j] + c)
@@ -302,47 +359,21 @@
     for j in range(1, K):
         small_copy(j).start()
     red_copy.wait_recv()
-    redt = (m.red_send[...] + m.red_recv[...]).astype(BF)
-    m.redt[...] = redt
-    dot_copy.wait_recv()
-    mean = jnp.sum(m.dot_send[...] + m.dot_recv[...], axis=1, keepdims=True) / QF
+    m.redt[...] = (m.red_send[...] + m.red_recv[...]).astype(BF)
+    back_copy.wait_recv()
+    back = m.back_send[...] + m.back_recv[...]
+    mean_row = back[ranks:ranks + 1, :] / QF
+    m.backt[...] = (back[0:ranks, :] - mean_row * m.base[...]).astype(BF)
+    mean = jnp.broadcast_to(mean_row, (LANES, T2)).T
     inv = m.inv[...]
-    m.coef[...] = inv * inv * jnp.broadcast_to(mean, (T2, LANES))
+    m.coef[...] = inv * inv * mean
 
     def rs_copy(i, j):
         return copy(m.rs_send[i].at[j - 1], m.rs_recv[i].at[j - 1],
                     m.rs_s.at[i], m.rs_r.at[i], d, 2 * chips[j] + c)
 
-    def whole(src, dst, ss, rs):
-        return copy(src, dst, ss, rs, d, sib)
-
-    back = jnp.zeros((ranks, T2), F32)
-    for js in (near, far + [0]):
-        for j in js:
-            k = chips[j]
-            inv, coef = wide(m.inv[...]), wide(m.coef[...])
-            for i in range(F // hw):
-                part = slice(i * hw, (i + 1) * hw)
-                p = m.p2[:, cols(k * F + i * hw, hw)].astype(F32)
-                delta = (inv * m.scaled[slot(j), :, part] - coef * p).astype(BF)
-                raising = adapt[k, :, W + i * hw:W + (i + 1) * hw]
-                back += lax.dot_general(raising, delta, NT, preferred_element_type=F32)
-                term = jnp.dot(m.redt[...], delta, preferred_element_type=F32)
-                if j == 0:
-                    m.own[0][:, part] = term
-                else:
-                    m.rs_send[0][j - 1, :, part] = term.astype(BF)
-        for j in js:
-            if j > 0:
-                rs_copy(0, j).start()
-    m.back_send[...] = back
-    back_copy.start()
-    back_copy.wait_recv()
-    m.backt[...] = (m.back_send[...] + m.back_recv[...]).astype(BF)
-
-    for i, (kind, off, width) in enumerate(pieces):
-        if kind == "u":
-            continue
+    last = len(pieces) - 1
+    for i, (kind, off, width) in enumerate(pieces[:last]):
         for j in list(range(1, K)) + [0]:
             term = jnp.dot(m.backt[...], m.a2[:, cols(chips[j] * W + off, width)], preferred_element_type=F32)
             if j == 0:
@@ -352,6 +383,40 @@
         for j in range(1, K):
             rs_copy(i, j).start()
 
+    for j in list(range(1, K)) + [0]:
+        k = chips[j]
+        coef = wide(m.coef[...])
+        for i in range(F // hw):
+            part = slice(i * hw, (i + 1) * hw)
+            p = m.p2[:, cols(k * F + i * hw, hw)].astype(F32)
+            delta = (m.scaled[slot(j), :, part] - coef * p).astype(BF)
+            term = jnp.dot(m.redt[...], delta, preferred_element_type=F32)
+            start = i * hw
+            if start < Z:
+                m.z_term[k, :, start:min(start + hw, Z)] = term[:, :min(hw, Z - start)]
+            if start + hw > Z:
+                rest = slice(max(start - Z, 0), start + hw - Z)
+                term = term[:, hw - (rest.stop - rest.start):]
+                if j == 0:
+                    m.own[last][:, rest] = term
+                else:
+                    m.rs_send[last][j - 1, :, rest] = term.astype(BF)
+    for j in range(1, K):
+        rs_copy(last, j).start()
+
+    def z_copy(k):
+        return copy(m.z_send.at[lax.rem(d + k, D)], m.z_recv.at[k - 1], m.z_s, m.z_r, lax.rem(d + k, D), s)
+
+    def z_share(j):
+        return copy(m.z_ag.at[chip], m.z_ag.at[chip], m.zag_s, m.zag_r, d, 2 * chips[j] + c)
+
+    if Z:
+        for e in range(D):
+            for k in range(K):
+                m.z_f[e, k * R:(k + 1) * R, :] = m.z_term[k, e * R:(e + 1) * R, :]
+            m.z_send[e] = m.z_f[e].astype(BF)
+        for k in range(1, D):
+            z_copy(k).start()
     small = m.small_send[0]
     small_all = whole(m.small_recv, m.small_recv, m.sm_s, m.sm_r)
     small_all.wait_recv()
@@ -389,7 +454,7 @@
 
     def put(i, q, value):
         kind, off, width = pieces[i]
-        out, base = (m.up_out, q * F) if kind == "u" else (m.down_out, q * W + off)
+        out, base = (m.up_out, q * F + off) if kind == "u" else (m.down_out, q * W + off)
 
         def store():
             where = cols(base, width)
@@ -420,6 +485,15 @@
 
     for i in range(len(pieces)):
         dp_stage(i)
+    if Z:
+        z_all = whole(m.z_send.at[0:D - 1], m.z_recv, m.z_s, m.z_r)
+        z_all.wait_recv()
+        total = m.z_f[d]
+        for k in range(1, D):
+            total += m.z_recv[k - 1].astype(F32)
+        m.z_ag[chip] = total.astype(BF)
+        for j in range(1, K):
+            z_share(j).start()
 
     small = m.small_dp[...]
     small_dp_all = whole(m.small_dp_recv, m.small_dp_recv, m.smd_s, m.smd_r)
@@ -443,11 +517,30 @@
         for n in range(groups):
             m.gain_out[:, cols(q * F + n * LANES, LANES)] = value[n:n + 1, :]
 
+    def put_z(core, total):
+        for q in range(K):
+            where = cols((2 * q + core) * F, Z)
+            for r in range(R):
+                m.up_out[r, :, where] = total[q * R + r:q * R + r + 1]
+
+    if Z:
+        z_shared = whole(m.z_ag.at[0:K - 1], m.z_ag.at[0:K - 1], m.zag_s, m.zag_r)
+        z_shared.wait_recv()
+        total = m.z_ag[0].astype(F32)
+        for q in range(1, K):
+            total += m.z_ag[q].astype(F32)
+        m.zx_send[...] = total
+        zx_copy = sib_copy(m.zx_send, m.zx_recv, 8)
+        zx_copy.start()
+        put_z(c, total * factor)
     put_gain(s, m.small_fin[...])
     small_ag_all = whole(m.small_ag, m.small_ag, m.sma_s, m.sma_r)
     small_ag_all.wait_recv()
     for j, cc in peers:
         put_gain(2 * frm(j) + other(cc), m.small_ag[2 * j + cc - 1])
+    if Z:
+        zx_copy.wait_recv()
+        put_z(1 - c, m.zx_recv[...] * factor)
     for i in range(len(pieces)):
         ag_all(i).wait_recv()
         for j, cc in peers:
@@ -456,8 +549,12 @@
     pos_copy(c).wait_send()
     valid_copy(c).wait_send()
     whole(m.cot_src, m.cot_src, m.cot_s, m.cot_r.at[0, 0]).wait_send()
-    for group in (sib_proj, sib_act, sq_copy, red_copy, dot_copy, back_copy,
-                  adapt_all, small_all, small_dp_all, small_ag_all):
+    if Z:
+        z_all.wait_send()
+        z_shared.wait_send()
+        zx_copy.wait_send()
+    for group in (sib_proj, sib_act, sq_copy, red_copy, base_copy, back_copy,
+                  raise_all, lower_all, small_all, small_dp_all, small_ag_all):
         group.wait_send()
     for i in range(len(pieces)):
         whole(m.rs_send[i], m.rs_recv[i], m.rs_s.at[i], m.rs_r.at[i]).wait_send()
@@ -495,8 +592,10 @@
     ranks = D * R
     folded = -(-K * R // 16) * 16
     first = -(-W // (2 * LANES)) * LANES
-    pieces = [("u", 0, F), ("d", 0, first)] + ([("d", first, W - first)] if W > first else [])
-    cfg = SimpleNamespace(S=S, D=D, T=T, F=F, W=W, R=R, RP=RP, M=M, QF=QF, KD=KD, tokens=D * S * T, pieces=pieces)
+    Z = F * 3 // (4 * LANES) * LANES if F >= 512 else 0
+    pieces = [("d", 0, first)] + ([("d", first, W - first)] if W > first else []) + [("u", Z, F - Z)]
+    cfg = SimpleNamespace(S=S, D=D, T=T, F=F, W=W, R=R, RP=RP, M=M, QF=QF, KD=KD, Z=Z,
+                          tokens=D * S * T, pieces=pieces)
 
     hw = 256 if F % 256 == 0 else 128
     small_rows = -(-(F // LANES + 1) // 8) * 8
@@ -515,9 +614,12 @@
         gains=vmem((1, QF), F32),
         swap=vmem((hw, hw), BF),
         fold=vmem((folded, W + F), F32),
-        packed=vmem((D, folded, W + F), BF),
-        adaptf=vmem((K, ranks, W + F), F32),
-        adapt=vmem((K, ranks, W + F), BF),
+        packed_r=vmem((D, folded, F), BF),
+        packed_l=vmem((D, folded, W), BF),
+        adaptf_r=vmem((K, ranks, F), F32),
+        adaptf_l=vmem((K, ranks, W), F32),
+        adapt_r=vmem((K, ranks, F), BF),
+        adapt_l=vmem((K, ranks, W), BF),
         scaled=vmem((K, T2, F), F32),
         cos=vmem((T2, LANES), F32),
         sin=vmem((T2, LANES), F32),
@@ -525,12 +627,15 @@
         coef=vmem((T2, LANES), F32),
         sq_send=vmem((T2, LANES), F32),
         sq_recv=vmem((T2, LANES), F32),
-        dot_send=vmem((T2, LANES), F32),
-        dot_recv=vmem((T2, LANES), F32),
+        dot=vmem((T2, LANES), F32),
+        inv_row=vmem((1, T2), F32),
+        base=vmem((ranks, T2), F32),
+        base_send=vmem((ranks, T2), F32),
+        base_recv=vmem((ranks, T2), F32),
         red_send=vmem((ranks, T2), F32),
         red_recv=vmem((ranks, T2), F32),
-        back_send=vmem((ranks, T2), F32),
-        back_recv=vmem((ranks, T2), F32),
+        back_send=vmem((ranks + 8, T2), F32),
+        back_recv=vmem((ranks + 8, T2), F32),
         redt=vmem((ranks, T2), BF),
         backt=vmem((ranks, T2), BF),
         small_send=vmem((K, small_rows, LANES), F32),
@@ -540,6 +645,16 @@
         small_fin=vmem((small_rows, LANES), F32),
         small_ag=vmem((S - 1, small_rows, LANES), F32),
     )
+    if Z:
+        scratch.update(
+            z_term=vmem((K, ranks, Z), F32),
+            z_f=vmem((D, folded, Z), F32),
+            z_send=vmem((D, folded, Z), BF),
+            z_recv=vmem((D - 1, folded, Z), BF),
+            z_ag=vmem((K, folded, Z), BF),
+            zx_send=vmem((folded, Z), F32),
+            zx_recv=vmem((folded, Z), F32),
+        )
     for kind, off, width in pieces:
         for name, value in dict(
             rs_send=vmem((K - 1, ranks, width), BF),
@@ -555,9 +670,9 @@
             scratch.setdefault(name, []).append(value)
     n = len(pieces)
     sems = dict(
-        local_sem=(10,), cot_s=(), cot_r=(K, 2), ad_s=(), ad_r=(), sib_s=(8,), sib_r=(8,),
+        local_sem=(10 + K,), cot_s=(), cot_r=(K, 2), ar_s=(), ar_r=(), al_s=(), al_r=(), sib_s=(9,), sib_r=(9,),
         sm_s=(), sm_r=(), smd_s=(), smd_r=(), sma_s=(), sma_r=(),
-        rs_s=(n,), rs_r=(n,), dp_s=(n,), dp_r=(n,), ag_s=(n,), ag_r=(n,),
+        z_s=(), z_r=(), zag_s=(), zag_r=(), rs_s=(n,), rs_r=(n,), dp_s=(n,), dp_r=(n,), ag_s=(n,), ag_r=(n,),
     )
     scratch.update({name: dma(shape) if shape else dma for name, shape in sems.items()})
     hbm = pl.BlockSpec(memory_space=pltpu.HBM)

time: 36.8 us -> 34.7 us (0.943)
  Pallas kernels: 36 us -> 33.9 us
    pallas_call x1, Pallas kernels: 35.2 us -> 33.1 us  [shards(): pl.pallas_call(functools.partial(kernel, cfg, tree), out_shape=leaves[len...]
where the time goes in v2:
time: 34.7 us; the launch traced here: 34.6 us
  Pallas kernels  33.9 us (98%)
  between operations  0.64 us (2%)
    pallas_call x1, Pallas kernels, shards(): pl.pallas_call(functools.partial(kernel, cfg, tree), out_shape=leaves[len...  33.1 us
    pallas_call x1, Pallas kernels, shards(): pl.pallas_call(write_out, out_shape=leaves[len(inputs):count], in_specs=[...  0.79 us

profile of v2, /device:TPU:0, one launch (start us, length us, event | category | flops | bytes accessed | tf_op | source)
XLA Modules:
  0.0 34.6 jit_solution(14197405797487940784)
XLA Ops:
  0.6 33.1 %shard_map.112 = (f32[12,1,5120]{2,1,0:T(1,128)S(1)}, f32[1,4096]{1,0:T(1,128)S(1)}, f32[12,1,4096]{2,1,0:T(1,128)S(1)}) custom-call(bf16[128,5120]{1,0:T(8,128)(2,1)} %bitcast.7, bf16[4,256,512]{2,1,0:T(8,128)(2,1)} %bitcast.8, f32[1,128]{1,0:T(1,128)} %constant.2.clone.refs_2_, f32[1,4096]{1,0:T(1,128)} %refs_3_.1, bf16[12,5120]{1,0:T(8,128)(2,1)} %bitcast.10, ...), custom_call_target="tpu_custom_call" | custom-call | tf_op jit(solution)/shard_map/pallas_call | solution.py:697
  33.8 0.8 %shard_map.113 = (f32[12,1,5120]{2,1,0:T(1,128)}, f32[1,4096]{1,0:T(1,128)}, f32[12,1,4096]{2,1,0:T(1,128)}) custom-call(f32[12,1,5120]{2,1,0:T(1,128)S(1)} %get-tuple-element.9.refs_0_, f32[1,4096]{1,0:T(1,128)S(1)} %get-tuple-element.10.refs_1_, f32[12,1,4096]{2,1,0:T(1,128)S(1)} %get-tuple-element.11.refs_2_), custom_call_target="tpu_custom_call" | custom-call | tf_op jit(solution)/shard_map/pallas_call | solution.py:707

commit v3 on v2

--- a/solution.py
+++ b/solution.py
@@ -34,7 +34,7 @@
     inputs, outputs, scratch = jax.tree.unflatten(tree, refs)
     m = SimpleNamespace(**inputs, **outputs, **scratch)
     S, D, T, F, W = cfg.S, cfg.D, cfg.T, cfg.F, cfg.W
-    R, RP, M, QF, KD, Z = cfg.R, cfg.RP, cfg.M, cfg.QF, cfg.KD, cfg.Z
+    R, M, QF, KD, Z = cfg.R, cfg.M, cfg.QF, cfg.KD, cfg.Z
     pieces = cfg.pieces
     K = S // 2
     T2 = 2 * T
@@ -47,6 +47,7 @@
     c = lax.rem(s, 2)
     chip = s // 2
     sib = s + 1 - 2 * c
+    par = 1 - c
 
     def to(j):
         if j == 0:
@@ -83,7 +84,7 @@
     def other(cc):
         return c if cc == 0 else 1 - c
 
-    peers = [(j, cc) for j in range(K) for cc in range(2) if (j, cc) != (0, 0)]
+    peers = [(j, cc) for j in reversed(range(K)) for cc in range(2) if (j, cc) != (0, 0)]
 
     barrier = pltpu.get_barrier_semaphore()
     for j, cc in peers:
@@ -94,40 +95,36 @@
     def local(src, dst, i):
         return pltpu.make_async_copy(src, dst, m.local_sem.at[i])
 
-    low_load = local(m.low_hbm, m.low, 0)
-    rai_load = local(m.rai_hbm, m.rai, 1)
-    pos_load = local(m.pos_hbm, m.pos.at[c], 2)
-    valid_load = local(m.valid_hbm, m.valid.at[c], 3)
-    freq_load = local(m.freq_hbm, m.freq, 4)
-    gains_load = local(m.gains_hbm, m.gains, 5)
-    cot_loads = [
-        local(m.cot_hbm.at[chips[j]], m.cot.at[0] if j == 0 else m.cot_src.at[j - 1], 10 + j)
-        for j in range(K)
-    ]
+    low_load = local(m.low_hbm, m.maps.at[:, 0:M], 0)
+    rai_load = local(m.rai_hbm, m.maps.at[:, M:M + QF], 0)
+    pos_load = local(m.pos_hbm, m.marks.at[c, 0:3], 1)
+    valid_load = local(m.valid_hbm, m.marks.at[c, 3], 1)
+    freq_load = local(m.freq_hbm, m.lines.at[:, 0:LANES], 2)
+    gains_load = local(m.gains_hbm, m.lines.at[:, LANES:LANES + QF], 2)
+    cot_loads = [local(m.cot_hbm.at[chips[j]], m.cot_src.at[j - 1], 4 + j) for j in range(1, K)]
     proj_loads = [
-        local(m.proj_hbm.at[:, cols((2 * k + c) * F, F)], m.p2.at[rows(c), pl.ds(k * F, F)], 8)
+        local(m.proj_hbm.at[:, cols((2 * k + par) * F, F)], m.p2.at[rows(c), pl.ds(k * F, F)], 3)
         for k in range(K)
     ]
     act_loads = [
-        local(m.act_hbm.at[:, cols((2 * k + c) * W, W)], m.a2.at[rows(c), pl.ds(k * W, W)], 9)
+        local(m.act_hbm.at[:, cols((2 * k + par) * W, W)], m.a2.at[rows(c), pl.ds(k * W, W)], 4)
         for k in range(KD)
     ]
     for j in range(1, K):
-        cot_loads[j].start()
+        cot_loads[j - 1].start()
     low_load.start()
     rai_load.start()
     pos_load.start()
     valid_load.start()
     freq_load.start()
     gains_load.start()
-    cot_loads[0].start()
     for load in proj_loads + act_loads:
         load.start()
 
     def cot_copy(j, r):
         part = pl.ds(r * T, T)
         return copy(m.cot_src.at[j - 1, part], m.cot.at[j, part],
-                    m.cot_s, m.cot_r.at[j, r], d, 2 * chips[j] + c)
+                    m.cot_s, m.cot_r.at[j - 1, r], d, 2 * chips[j] + par)
 
     def raise_copy(k):
         return copy(m.packed_r.at[d], m.packed_r.at[d], m.ar_s, m.ar_r, lax.rem(d + k, D), s)
@@ -138,18 +135,21 @@
     def sib_copy(src, dst, i):
         return copy(src, dst, m.sib_s.at[i], m.sib_r.at[i], d, sib)
 
+    def own_copy():
+        return sib_copy(m.cot_hbm.at[chip], m.cot.at[0], 6)
+
     def pos_copy(core):
-        return sib_copy(m.pos_hbm, m.pos.at[core], 0)
+        return sib_copy(m.pos_hbm, m.marks.at[core, 0:3], 0)
 
     def valid_copy(core):
-        return sib_copy(m.valid_hbm, m.valid.at[core], 1)
+        return sib_copy(m.valid_hbm, m.marks.at[core, 3], 0)
 
     def proj_copy(k, core):
-        return sib_copy(m.proj_hbm.at[:, cols((2 * k + 1 - c) * F, F)],
+        return sib_copy(m.proj_hbm.at[:, cols((2 * k + c) * F, F)],
                         m.p2.at[rows(core), pl.ds(k * F, F)], 6)
 
     def act_copy(k, core):
-        return sib_copy(m.act_hbm.at[:, cols((2 * k + 1 - c) * W, W)],
+        return sib_copy(m.act_hbm.at[:, cols((2 * k + c) * W, W)],
                         m.a2.at[rows(core), pl.ds(k * W, W)], 7)
 
     def xch_copy(send, recv, i):
@@ -168,30 +168,27 @@
     pos_copy(c).start()
     valid_copy(c).start()
     for j in near:
-        cot_loads[j].wait()
+        cot_loads[j - 1].wait()
         cot_copy(j, 0).start()
     for j in near:
         cot_copy(j, 1).start()
     for j in far:
-        cot_loads[j].wait()
-
-    def far_sends():
-        for j in far:
-            for r in range(2):
-                cot_copy(j, r).start()
-
-    pl.when(c == 0)(far_sends)
+        cot_loads[j - 1].wait()
+
+    for j in far:
+        for r in range(2):
+            cot_copy(j, r).start()
+    own_copy().start()
     fold = m.fold
     if fold.shape[0] > K * R or KD < K:
         fold[...] = jnp.zeros_like(fold)
     if KD < K:
         m.a2[:, KD * W:] = jnp.zeros((T2, (K - KD) * W), BF)
-    low_load.wait()
-    rai_load.wait()
+    local(m.maps, m.maps, 0).wait()
     for q in range(K):
         if q < KD:
-            fold[q * R:(q + 1) * R, 0:W] = m.low[:, cols((2 * q + c) * W, W)].astype(F32)
-        fold[q * R:(q + 1) * R, W:W + F] = m.rai[:, cols((2 * q + c) * F, F)].astype(F32)
+            fold[q * R:(q + 1) * R, 0:W] = m.maps[:, cols((2 * q + par) * W, W)].astype(F32)
+        fold[q * R:(q + 1) * R, W:W + F] = m.maps[:, cols(M + (2 * q + par) * F, F)].astype(F32)
     m.packed_r[d] = fold[:, W:].astype(BF)
     m.packed_l[d] = fold[:, :W].astype(BF)
 
@@ -211,12 +208,10 @@
         even & (row_i == col_i + 1), 1.0, jnp.where(jnp.logical_not(even) & (row_i == col_i - 1), -1.0, 0.0)
     ).astype(BF)
 
-    pos_load.wait()
-    valid_load.wait()
-    freq_load.wait()
-    gains_load.wait()
-    pos_copy(1 - c).wait_recv()
-    valid_copy(1 - c).wait_recv()
+    local(m.marks.at[c], m.marks.at[c], 1).wait()
+    local(m.lines, m.lines, 2).wait()
+    sib_marks = sib_copy(m.marks.at[c], m.marks.at[1 - c], 0)
+    sib_marks.wait_recv()
     n0, n1, _ = group_counts()
     lane = lax.broadcasted_iota(jnp.int32, (T, LANES), 1)
 
@@ -226,19 +221,19 @@
     count = jnp.zeros((1, 1), F32)
     for h in range(2):
         index = jnp.where(
-            lane < 2 * n0, column(m.pos[h, 0]),
-            jnp.where(lane < 2 * (n0 + n1), column(m.pos[h, 1]), column(m.pos[h, 2])),
+            lane < 2 * n0, column(m.marks[h, 0]),
+            jnp.where(lane < 2 * (n0 + n1), column(m.marks[h, 1]), column(m.marks[h, 2])),
         )
-        angle = index * m.freq[...]
-        ok = column(m.valid[h])
+        angle = index * m.lines[:, 0:LANES]
+        ok = column(m.marks[h, 3])
         m.cos[h * T:(h + 1) * T, :] = jnp.cos(angle) * ok
         m.sin[h * T:(h + 1) * T, :] = jnp.sin(angle) * ok
-        count += jnp.sum(m.valid[h].astype(F32), axis=1, keepdims=True)
+        count += jnp.sum(m.marks[h, 3].astype(F32), axis=1, keepdims=True)
     m.small_send[...] = jnp.broadcast_to(count[:, :, None], m.small_send.shape)
 
     proj_all = m.proj_hbm.at[:, 0:K * F]
-    local(proj_all, m.p2.at[rows(c)], 8).wait()
-    sib_proj = sib_copy(proj_all, m.p2.at[rows(1 - c)], 6)
+    local(proj_all, m.p2.at[rows(c)], 3).wait()
+    sib_proj = sib_copy(m.cot.at[0:(K + 2) // 2], m.cot.at[0:(K + 2) // 2], 6)
     sib_proj.wait_recv()
     square = jnp.zeros((T2, LANES), F32)
     for i in range(K * groups):
@@ -247,7 +242,6 @@
     m.sq_send[...] = square
     sq_copy.start()
     m.dot[...] = jnp.zeros_like(m.dot)
-    cot_loads[0].wait()
     sq_copy.wait_recv()
     square = m.sq_send[...] + m.sq_recv[...]
     inverse = lax.rsqrt(jnp.sum(square, axis=1, keepdims=True) / QF + EPSILON)
@@ -275,7 +269,7 @@
                 if r > 0:
                     piece += m.small_send[j, n:n + 1, :]
                 m.small_send[j, n:n + 1, :] = piece
-            gn = m.gains[:, cols((2 * k + c) * F + i * hw, hw)]
+            gn = m.lines[:, cols(LANES + (2 * k + par) * F + i * hw, hw)]
             m.scaled[j, part, i * hw:(i + 1) * hw] = un * gn * inv
             pg = prod * gn
             acc = pg[:, :LANES]
@@ -306,10 +300,8 @@
     chunk(0, 0)
     chunk(0, 1)
     split = 2 * len(near)
-    for (j, r), n in zip(order[:split], range(split)):
+    for j, r in order[:split]:
         cot_copy(j, r).wait_recv()
-        if n == 2:
-            pl.when(c == 1)(far_sends)
         chunk(j, r)
     raise_all = whole(m.packed_r.at[0:D - 1], m.packed_r.at[0:D - 1], m.ar_s, m.ar_r)
     raise_all.wait_recv()
@@ -333,7 +325,7 @@
     lower_all.wait_recv()
     unfold(m.packed_l, m.adaptf_l, m.adapt_l)
     act_all = m.act_hbm.at[:, 0:KD * W]
-    local(act_all, m.a2.at[rows(c), 0:KD * W], 9).wait()
+    local(act_all, m.a2.at[rows(c), 0:KD * W], 4).wait()
     sib_act = sib_copy(act_all, m.a2.at[rows(1 - c), 0:KD * W], 7)
     sib_act.wait_recv()
     red = jnp.zeros((ranks, T2), F32)
@@ -373,16 +365,23 @@
                     m.rs_s.at[i], m.rs_r.at[i], d, 2 * chips[j] + c)
 
     last = len(pieces) - 1
-    for i, (kind, off, width) in enumerate(pieces[:last]):
-        for j in list(range(1, K)) + [0]:
-            term = jnp.dot(m.backt[...], m.a2[:, cols(chips[j] * W + off, width)], preferred_element_type=F32)
-            if j == 0:
-                m.own[i][...] = term
-            else:
-                m.rs_send[i][j - 1] = term.astype(BF)
-        for j in range(1, K):
-            rs_copy(i, j).start()
-
+    def store_term(i, j, lanes, term):
+        if j == 0:
+            m.own[i][:, lanes] = term
+        else:
+            m.rs_send[i][j - 1, :, lanes] = term.astype(BF)
+
+    for i, (off, end) in enumerate(pieces):
+        width = min(end, W) - off
+        if width > 0:
+            for j in list(range(1, K)) + [0]:
+                values = m.a2[:, cols(chips[j] * W + off, width)]
+                store_term(i, j, slice(0, width), jnp.dot(m.backt[...], values, preferred_element_type=F32))
+        if i < last:
+            for j in far + near:
+                rs_copy(i, j).start()
+
+    up_lane = W - pieces[last][0]
     for j in list(range(1, K)) + [0]:
         k = chips[j]
         coef = wide(m.coef[...])
@@ -395,17 +394,15 @@
             if start < Z:
                 m.z_term[k, :, start:min(start + hw, Z)] = term[:, :min(hw, Z - start)]
             if start + hw > Z:
-                rest = slice(max(start - Z, 0), start + hw - Z)
-                term = term[:, hw - (rest.stop - rest.start):]
-                if j == 0:
-                    m.own[last][:, rest] = term
-                else:
-                    m.rs_send[last][j - 1, :, rest] = term.astype(BF)
-    for j in range(1, K):
+                first = max(start - Z, 0)
+                width = start + hw - Z - first
+                lanes = slice(up_lane + first, up_lane + first + width)
+                store_term(last, j, lanes, term[:, hw - width:])
+    for j in far + near:
         rs_copy(last, j).start()
 
     def z_copy(k):
-        return copy(m.z_send.at[lax.rem(d + k, D)], m.z_recv.at[k - 1], m.z_s, m.z_r, lax.rem(d + k, D), s)
+        return copy(m.z_send.at[lax.rem(d + k, D)], m.z_recv.at[k - 1], m.z_s, m.z_r, lax.rem(d + k, D), sib)
 
     def z_share(j):
         return copy(m.z_ag.at[chip], m.z_ag.at[chip], m.zag_s, m.zag_r, d, 2 * chips[j] + c)
@@ -417,6 +414,8 @@
             m.z_send[e] = m.z_f[e].astype(BF)
         for k in range(1, D):
             z_copy(k).start()
+        z_own = sib_copy(m.z_f.at[d], m.z_own, 1)
+        z_own.start()
     small = m.small_send[0]
     small_all = whole(m.small_recv, m.small_recv, m.sm_s, m.sm_r)
     small_all.wait_recv()
@@ -432,7 +431,10 @@
 
     def dp_copy(i, k):
         return copy(m.dp_send[i].at[lax.rem(d + k, D)], m.dp_recv[i].at[k - 1],
-                    m.dp_s.at[i], m.dp_r.at[i], lax.rem(d + k, D), s)
+                    m.dp_s.at[i], m.dp_r.at[i], lax.rem(d + k, D), sib)
+
+    def dp_own(i):
+        return sib_copy(m.dp_f[i].at[d], m.dp_own[i], 11 + i)
 
     def dp_stage(i):
         total = m.own[i][...]
@@ -440,44 +442,58 @@
         for j in range(1, K):
             total += m.rs_recv[i][j - 1].astype(F32)
         tot = m.tot[i]
-        tot[0:ranks, :] = total
+        tot[...] = total
         for e in range(D):
-            block = tot[e * R:e * R + RP, :]
-            m.dp_f[i][e] = block
-            m.dp_send[i][e] = block.astype(BF)
+            for b in range(tot.shape[1] // LANES):
+                part = tot[e * R:(e + 1) * R, b * LANES:(b + 1) * LANES]
+                m.dp_f[i][e, b * R:(b + 1) * R, :] = part
+            m.dp_send[i][e] = m.dp_f[i][e].astype(BF)
         for k in range(1, D):
             dp_copy(i, k).start()
+        dp_own(i).start()
 
     def ag_copy(i, j, cc):
-        return copy(m.fin[i], m.ag[i].at[2 * j + cc - 1], m.ag_s.at[i], m.ag_r.at[i],
+        return copy(m.fin[i], m.ag[i].at[2 * j + cc - 1], m.ag_s.at[i - 1], m.ag_r.at[i - 1],
                     d, 2 * chips[j] + other(cc))
 
     def put(i, q, value):
-        kind, off, width = pieces[i]
-        out, base = (m.up_out, q * F + off) if kind == "u" else (m.down_out, q * W + off)
-
-        def store():
-            where = cols(base, width)
-            for r in range(R):
-                out[r, :, where] = value[r:r + 1]
-
-        if kind == "d" and S * W != M:
-            pl.when(base + width <= M)(store)
-        else:
-            store()
+        off, end = pieces[i]
+        for b in range((end - off) // LANES):
+            lane = off + b * LANES
+            block = value[b * R:(b + 1) * R]
+
+            def store(out, base, block=block):
+                out[:, 0, cols(base, LANES)] = block
+
+            if lane >= W:
+                store(m.up_out, q * F + Z + lane - W)
+            elif S * W == M:
+                store(m.down_out, q * W + lane)
+            else:
+                base = q * W + lane
+                pl.when(base + LANES <= M)(functools.partial(store, m.down_out, base))
 
     def dp_all(i):
         return whole(m.dp_send[i].at[0:D - 1], m.dp_recv[i], m.dp_s.at[i], m.dp_r.at[i])
 
     def ag_all(i):
-        return whole(m.ag[i], m.ag[i], m.ag_s.at[i], m.ag_r.at[i])
+        return whole(m.ag[i], m.ag[i], m.ag_s.at[i - 1], m.ag_r.at[i - 1])
+
+    def ring_copy(j):
+        return copy(m.ring.at[chip], m.ring.at[chip], m.ring_s, m.ring_r, d, 2 * chips[j] + c)
 
     def gather(i, factor):
-        total = m.dp_f[i][d]
+        dp_own(i).wait_recv()
+        total = m.dp_own[i][...]
         dp_all(i).wait_recv()
         for k in range(1, D):
             total += m.dp_recv[i][k - 1].astype(F32)
         fin = (total * factor).astype(BF)
+        if i == 0:
+            m.ring[chip] = fin
+            for j in far + near:
+                ring_copy(j).start()
+            return
         m.fin[i][...] = fin
         for j, cc in peers:
             ag_copy(i, j, cc).start()
@@ -488,11 +504,12 @@
     if Z:
         z_all = whole(m.z_send.at[0:D - 1], m.z_recv, m.z_s, m.z_r)
         z_all.wait_recv()
-        total = m.z_f[d]
+        z_own.wait_recv()
+        total = m.z_own[...]
         for k in range(1, D):
             total += m.z_recv[k - 1].astype(F32)
         m.z_ag[chip] = total.astype(BF)
-        for j in range(1, K):
+        for j in far + near:
             z_share(j).start()
 
     small = m.small_dp[...]
@@ -501,14 +518,13 @@
     for k in range(1, D):
         small += m.small_dp_recv[k - 1]
     factor = F32(cfg.tokens) / small[groups:groups + 1, 0:1]
-    m.small_fin[...] = small * factor
-
-    def small_ag_copy(j, cc):
-        return copy(m.small_fin, m.small_ag.at[2 * j + cc - 1], m.sma_s, m.sma_r,
-                    d, 2 * chips[j] + other(cc))
-
-    for j, cc in peers:
-        small_ag_copy(j, cc).start()
+    m.small_ag[chip] = small * factor
+
+    def small_ag_copy(j):
+        return copy(m.small_ag.at[chip], m.small_ag.at[chip], m.sma_s, m.sma_r, d, 2 * chips[j] + c)
+
+    for j in far + near:
+        small_ag_copy(j).start()
 
     for i in range(len(pieces)):
         gather(i, factor)
@@ -519,9 +535,7 @@
 
     def put_z(core, total):
         for q in range(K):
-            where = cols((2 * q + core) * F, Z)
-            for r in range(R):
-                m.up_out[r, :, where] = total[q * R + r:q * R + r + 1]
+            m.up_out[:, 0, cols((2 * q + core) * F, Z)] = total[q * R:(q + 1) * R]
 
     if Z:
         z_shared = whole(m.z_ag.at[0:K - 1], m.z_ag.at[0:K - 1], m.zag_s, m.zag_r)
@@ -533,33 +547,48 @@
         zx_copy = sib_copy(m.zx_send, m.zx_recv, 8)
         zx_copy.start()
         put_z(c, total * factor)
-    put_gain(s, m.small_fin[...])
-    small_ag_all = whole(m.small_ag, m.small_ag, m.sma_s, m.sma_r)
+    small_ag_all = whole(m.small_ag.at[0:K - 1], m.small_ag.at[0:K - 1], m.sma_s, m.sma_r)
     small_ag_all.wait_recv()
-    for j, cc in peers:
-        put_gain(2 * frm(j) + other(cc), m.small_ag[2 * j + cc - 1])
+    small_pass = sib_copy(m.small_ag, m.small_pass, 9)
+    small_pass.start()
+    for q in range(K):
+        put_gain(2 * q + par, m.small_ag[q])
+    ring_all = whole(m.ring.at[0:K - 1], m.ring.at[0:K - 1], m.ring_s, m.ring_r)
+    ring_all.wait_recv()
+    ring_pass = sib_copy(m.ring, m.ring_pass, 10)
+    ring_pass.start()
+    for q in range(K):
+        put(0, 2 * q + c, m.ring[q].astype(F32))
     if Z:
         zx_copy.wait_recv()
         put_z(1 - c, m.zx_recv[...] * factor)
-    for i in range(len(pieces)):
+    small_pass.wait_recv()
+    for q in range(K):
+        put_gain(2 * q + c, m.small_pass[q])
+    for i in range(1, len(pieces)):
         ag_all(i).wait_recv()
         for j, cc in peers:
             put(i, 2 * frm(j) + other(cc), m.ag[i][2 * j + cc - 1].astype(F32))
-
-    pos_copy(c).wait_send()
-    valid_copy(c).wait_send()
+    ring_pass.wait_recv()
+    for q in range(K):
+        put(0, 2 * q + par, m.ring_pass[q].astype(F32))
+
+    sib_marks.wait_send()
     whole(m.cot_src, m.cot_src, m.cot_s, m.cot_r.at[0, 0]).wait_send()
     if Z:
         z_all.wait_send()
         z_shared.wait_send()
         zx_copy.wait_send()
+        z_own.wait_send()
     for group in (sib_proj, sib_act, sq_copy, red_copy, base_copy, back_copy,
-                  raise_all, lower_all, small_all, small_dp_all, small_ag_all):
+                  ring_all, ring_pass, small_pass, raise_all, lower_all, small_all, small_dp_all, small_ag_all):
         group.wait_send()
     for i in range(len(pieces)):
         whole(m.rs_send[i], m.rs_recv[i], m.rs_s.at[i], m.rs_r.at[i]).wait_send()
         dp_all(i).wait_send()
-        ag_all(i).wait_send()
+        dp_own(i).wait_send()
+        if i > 0:
+            ag_all(i).wait_send()
 
 
 def write_out(*refs):
@@ -586,15 +615,15 @@
     R, M = adapter_lowering.shape[1:]
     W = block_width(M, S)
     KD = M // (2 * W)
-    RP = -(-R // 16) * 16
     K = S // 2
     T2 = 2 * T
     ranks = D * R
     folded = -(-K * R // 16) * 16
-    first = -(-W // (2 * LANES)) * LANES
     Z = F * 3 // (4 * LANES) * LANES if F >= 512 else 0
-    pieces = [("d", 0, first)] + ([("d", first, W - first)] if W > first else []) + [("u", Z, F - Z)]
-    cfg = SimpleNamespace(S=S, D=D, T=T, F=F, W=W, R=R, RP=RP, M=M, QF=QF, KD=KD, Z=Z,
+    starts = list(range(0, W - 2 * LANES + 1, 2 * LANES))
+    starts.append(starts[-1] + 2 * LANES if starts else 0)
+    pieces = list(zip(starts, starts[1:] + [W + F - Z]))
+    cfg = SimpleNamespace(S=S, D=D, T=T, F=F, W=W, R=R, M=M, QF=QF, KD=KD, Z=Z,
                           tokens=D * S * T, pieces=pieces)
 
     hw = 256 if F % 256 == 0 else 128
@@ -606,12 +635,9 @@
         a2=vmem((T2, K * W), BF),
         cot=vmem((K, T2, F), BF),
         cot_src=vmem((K - 1, T2, F), BF),
-        low=vmem((R, M), BF),
-        rai=vmem((R, QF), BF),
-        pos=vmem((2, 3, 1, T), jnp.int32),
-        valid=vmem((2, 1, T), jnp.int32),
-        freq=vmem((1, LANES), F32),
-        gains=vmem((1, QF), F32),
+        maps=vmem((R, M + QF), BF),
+        marks=vmem((2, 4, 1, T), jnp.int32),
+        lines=vmem((1, LANES + QF), F32),
         swap=vmem((hw, hw), BF),
         fold=vmem((folded, W + F), F32),
         packed_r=vmem((D, folded, F), BF),
@@ -642,8 +668,8 @@
         small_recv=vmem((K - 1, small_rows, LANES), F32),
         small_dp=vmem((small_rows, LANES), F32),
         small_dp_recv=vmem((D - 1, small_rows, LANES), F32),
-        small_fin=vmem((small_rows, LANES), F32),
-        small_ag=vmem((S - 1, small_rows, LANES), F32),
+        small_ag=vmem((K, small_rows, LANES), F32),
+        small_pass=vmem((K, small_rows, LANES), F32),
     )
     if Z:
         scratch.update(
@@ -652,27 +678,33 @@
             z_send=vmem((D, folded, Z), BF),
             z_recv=vmem((D - 1, folded, Z), BF),
             z_ag=vmem((K, folded, Z), BF),
+            z_own=vmem((folded, Z), F32),
             zx_send=vmem((folded, Z), F32),
             zx_recv=vmem((folded, Z), F32),
         )
-    for kind, off, width in pieces:
+    for off, end in pieces:
+        width = end - off
+        rows = -(-R * (width // LANES) // 8) * 8
         for name, value in dict(
             rs_send=vmem((K - 1, ranks, width), BF),
             rs_recv=vmem((K - 1, ranks, width), BF),
             own=vmem((ranks, width), F32),
-            tot=vmem((ranks + RP, width), F32),
-            dp_f=vmem((D, RP, width), F32),
-            dp_send=vmem((D, RP, width), BF),
-            dp_recv=vmem((D - 1, RP, width), BF),
-            fin=vmem((RP, width), BF),
-            ag=vmem((S - 1, RP, width), BF),
+            tot=vmem((ranks, width), F32),
+            dp_f=vmem((D, rows, LANES), F32),
+            dp_send=vmem((D, rows, LANES), BF),
+            dp_own=vmem((rows, LANES), F32),
+            dp_recv=vmem((D - 1, rows, LANES), BF),
+            fin=vmem((rows, LANES), BF),
+            ag=vmem((S - 1, rows, LANES), BF),
         ).items():
             scratch.setdefault(name, []).append(value)
+    ring = vmem((K, -(-R * (pieces[0][1] // LANES) // 8) * 8, LANES), BF)
+    scratch.update(ring=ring, ring_pass=ring)
     n = len(pieces)
     sems = dict(
-        local_sem=(10 + K,), cot_s=(), cot_r=(K, 2), ar_s=(), ar_r=(), al_s=(), al_r=(), sib_s=(9,), sib_r=(9,),
+        local_sem=(4 + K,), cot_s=(), cot_r=(K - 1, 2), ar_s=(), ar_r=(), al_s=(), al_r=(), sib_s=(11 + n,), sib_r=(11 + n,), ring_s=(), ring_r=(),
         sm_s=(), sm_r=(), smd_s=(), smd_r=(), sma_s=(), sma_r=(),
-        z_s=(), z_r=(), zag_s=(), zag_r=(), rs_s=(n,), rs_r=(n,), dp_s=(n,), dp_r=(n,), ag_s=(n,), ag_r=(n,),
+        z_s=(), z_r=(), zag_s=(), zag_r=(), rs_s=(n,), rs_r=(n,), dp_s=(n,), dp_r=(n,), ag_s=(n - 1,), ag_r=(n - 1,),
     )
     scratch.update({name: dma(shape) if shape else dma for name, shape in sems.items()})
     hbm = pl.BlockSpec(memory_space=pltpu.HBM)

time: 34.7 us -> 33.9 us (0.977)
  Pallas kernels: 33.9 us -> 33.1 us
    pallas_call x1, Pallas kernels: 33.1 us -> 32.3 us  [shards(): pl.pallas_call(functools.partial(kernel, cfg, tree), out_shape=leaves[len...]
where the time goes in v3:
time: 33.9 us; the launch traced here: 33.7 us
  Pallas kernels  33.1 us (98%)
  between operations  0.64 us (2%)
    pallas_call x1, Pallas kernels, shards(): pl.pallas_call(functools.partial(kernel, cfg, tree), out_shape=leaves[len...  32.3 us
    pallas_call x1, Pallas kernels, shards(): pl.pallas_call(write_out, out_shape=leaves[len(inputs):count], in_specs=[...  0.79 us

profile of v3, /device:TPU:0, one launch (start us, length us, event | category | flops | bytes accessed | tf_op | source)
XLA Modules:
  0.0 33.7 jit_solution(147156193841448849)
XLA Ops:
  0.6 32.3 %shard_map.112 = (f32[12,1,5120]{2,1,0:T(1,128)S(1)}, f32[1,4096]{1,0:T(1,128)S(1)}, f32[12,1,4096]{2,1,0:T(1,128)S(1)}) custom-call(bf16[128,5120]{1,0:T(8,128)(2,1)} %bitcast.7, bf16[4,256,512]{2,1,0:T(8,128)(2,1)} %bitcast.8, f32[1,128]{1,0:T(1,128)} %constant.2.clone.refs_2_, f32[1,4096]{1,0:T(1,128)} %refs_3_.1, bf16[12,5120]{1,0:T(8,128)(2,1)} %bitcast.10, ...), custom_call_target="tpu_custom_call" | custom-call | tf_op jit(solution)/shard_map/pallas_call | solution.py:729
  33.0 0.8 %shard_map.113 = (f32[12,1,5120]{2,1,0:T(1,128)}, f32[1,4096]{1,0:T(1,128)}, f32[12,1,4096]{2,1,0:T(1,128)}) custom-call(f32[12,1,5120]{2,1,0:T(1,128)S(1)} %get-tuple-element.9.refs_0_, f32[1,4096]{1,0:T(1,128)S(1)} %get-tuple-element.10.refs_1_, f32[12,1,4096]{2,1,0:T(1,128)S(1)} %get-tuple-element.11.refs_2_), custom_call_target="tpu_custom_call" | custom-call | tf_op jit(solution)/shard_map/pallas_call | solution.py:739

commit v4 on v3

--- a/solution.py
+++ b/solution.py
@@ -184,6 +184,7 @@
         fold[...] = jnp.zeros_like(fold)
     if KD < K:
         m.a2[:, KD * W:] = jnp.zeros((T2, (K - KD) * W), BF)
+
     local(m.maps, m.maps, 0).wait()
     for q in range(K):
         if q < KD:
@@ -233,6 +234,7 @@
 
     proj_all = m.proj_hbm.at[:, 0:K * F]
     local(proj_all, m.p2.at[rows(c)], 3).wait()
+
     sib_proj = sib_copy(m.cot.at[0:(K + 2) // 2], m.cot.at[0:(K + 2) // 2], 6)
     sib_proj.wait_recv()
     square = jnp.zeros((T2, LANES), F32)
@@ -407,6 +409,19 @@
     def z_share(j):
         return copy(m.z_ag.at[chip], m.z_ag.at[chip], m.zag_s, m.zag_r, d, 2 * chips[j] + c)
 
+    small = m.small_send[0]
+    small_all = whole(m.small_recv, m.small_recv, m.sm_s, m.sm_r)
+    small_all.wait_recv()
+    for j in range(1, K):
+        small += m.small_recv[j - 1]
+    m.small_dp[...] = small
+
+    def small_dp_copy(k):
+        return copy(m.small_dp, m.small_dp_recv.at[k - 1], m.smd_s, m.smd_r, lax.rem(d + k, D), s)
+
+    for k in range(1, D):
+        small_dp_copy(k).start()
+
     if Z:
         for e in range(D):
             for k in range(K):
@@ -416,18 +431,6 @@
             z_copy(k).start()
         z_own = sib_copy(m.z_f.at[d], m.z_own, 1)
         z_own.start()
-    small = m.small_send[0]
-    small_all = whole(m.small_recv, m.small_recv, m.sm_s, m.sm_r)
-    small_all.wait_recv()
-    for j in range(1, K):
-        small += m.small_recv[j - 1]
-    m.small_dp[...] = small
-
-    def small_dp_copy(k):
-        return copy(m.small_dp, m.small_dp_recv.at[k - 1], m.smd_s, m.smd_r, lax.rem(d + k, D), s)
-
-    for k in range(1, D):
-        small_dp_copy(k).start()
 
     def dp_copy(i, k):
         return copy(m.dp_send[i].at[lax.rem(d + k, D)], m.dp_recv[i].at[k - 1],

time: 33.9 us -> 33.6 us (level)
  no operation moved by 1% of the time
where the time goes in v4:
time: 33.6 us; the launch traced here: 33.5 us
  Pallas kernels  32.9 us (98%)
  between operations  0.64 us (2%)
    pallas_call x1, Pallas kernels, shards(): pl.pallas_call(functools.partial(kernel, cfg, tree), out_shape=leaves[len...  32.1 us
    pallas_call x1, Pallas kernels, shards(): pl.pallas_call(write_out, out_shape=leaves[len(inputs):count], in_specs=[...  0.79 us

profile of v4, /device:TPU:0, one launch (start us, length us, event | category | flops | bytes accessed | tf_op | source)
XLA Modules:
  0.0 33.5 jit_solution(10663103056958694225)
XLA Ops:
  0.6 32.1 %shard_map.112 = (f32[12,1,5120]{2,1,0:T(1,128)S(1)}, f32[1,4096]{1,0:T(1,128)S(1)}, f32[12,1,4096]{2,1,0:T(1,128)S(1)}) custom-call(bf16[128,5120]{1,0:T(8,128)(2,1)} %bitcast.7, bf16[4,256,512]{2,1,0:T(8,128)(2,1)} %bitcast.8, f32[1,128]{1,0:T(1,128)} %constant.2.clone.refs_2_, f32[1,4096]{1,0:T(1,128)} %refs_3_.1, bf16[12,5120]{1,0:T(8,128)(2,1)} %bitcast.10, ...), custom_call_target="tpu_custom_call" | custom-call | tf_op jit(solution)/shard_map/pallas_call | solution.py:732
  32.7 0.8 %shard_map.113 = (f32[12,1,5120]{2,1,0:T(1,128)}, f32[1,4096]{1,0:T(1,128)}, f32[12,1,4096]{2,1,0:T(1,128)}) custom-call(f32[12,1,5120]{2,1,0:T(1,128)S(1)} %get-tuple-element.9.refs_0_, f32[1,4096]{1,0:T(1,128)S(1)} %get-tuple-element.10.refs_1_, f32[12,1,4096]{2,1,0:T(1,128)S(1)} %get-tuple-element.11.refs_2_), custom_call_target="tpu_custom_call" | custom-call | tf_op jit(solution)/shard_map/pallas_call | solution.py:742

commit v5 on v4

--- a/solution.py
+++ b/solution.py
@@ -373,12 +373,15 @@
         else:
             m.rs_send[i][j - 1, :, lanes] = term.astype(BF)
 
+    def down_term(i, j, off, width):
+        values = m.a2[:, cols(chips[j] * W + off, width)]
+        store_term(i, j, slice(0, width), jnp.dot(m.backt[...], values, preferred_element_type=F32))
+
     for i, (off, end) in enumerate(pieces):
         width = min(end, W) - off
         if width > 0:
-            for j in list(range(1, K)) + [0]:
-                values = m.a2[:, cols(chips[j] * W + off, width)]
-                store_term(i, j, slice(0, width), jnp.dot(m.backt[...], values, preferred_element_type=F32))
+            for j in far + near:
+                down_term(i, j, off, width)
         if i < last:
             for j in far + near:
                 rs_copy(i, j).start()
@@ -402,6 +405,9 @@
                 store_term(last, j, lanes, term[:, hw - width:])
     for j in far + near:
         rs_copy(last, j).start()
+    for i, (off, end) in enumerate(pieces):
+        if off < W:
+            down_term(i, 0, off, min(end, W) - off)
 
     def z_copy(k):
         return copy(m.z_send.at[lax.rem(d + k, D)], m.z_recv.at[k - 1], m.z_s, m.z_r, lax.rem(d + k, D), sib)

time: 33.6 us -> 33.6 us (level)
  no operation moved by 1% of the time
where the time goes in v5:
time: 33.6 us; the launch traced here: 33.5 us
  Pallas kernels  32.9 us (98%)
  between operations  0.64 us (2%)
    pallas_call x1, Pallas kernels, shards(): pl.pallas_call(functools.partial(kernel, cfg, tree), out_shape=leaves[len...  32.1 us
    pallas_call x1, Pallas kernels, shards(): pl.pallas_call(write_out, out_shape=leaves[len(inputs):count], in_specs=[...  0.79 us

profile of v5, /device:TPU:0, one launch (start us, length us, event | category | flops | bytes accessed | tf_op | source)
XLA Modules:
  0.0 33.5 jit_solution(14182983080835377795)
XLA Ops:
  0.6 32.1 %shard_map.112 = (f32[12,1,5120]{2,1,0:T(1,128)S(1)}, f32[1,4096]{1,0:T(1,128)S(1)}, f32[12,1,4096]{2,1,0:T(1,128)S(1)}) custom-call(bf16[128,5120]{1,0:T(8,128)(2,1)} %bitcast.7, bf16[4,256,512]{2,1,0:T(8,128)(2,1)} %bitcast.8, f32[1,128]{1,0:T(1,128)} %constant.2.clone.refs_2_, f32[1,4096]{1,0:T(1,128)} %refs_3_.1, bf16[12,5120]{1,0:T(8,128)(2,1)} %bitcast.10, ...), custom_call_target="tpu_custom_call" | custom-call | tf_op jit(solution)/shard_map/pallas_call | solution.py:738
  32.7 0.8 %shard_map.113 = (f32[12,1,5120]{2,1,0:T(1,128)}, f32[1,4096]{1,0:T(1,128)}, f32[12,1,4096]{2,1,0:T(1,128)}) custom-call(f32[12,1,5120]{2,1,0:T(1,128)S(1)} %get-tuple-element.9.refs_0_, f32[1,4096]{1,0:T(1,128)S(1)} %get-tuple-element.10.refs_1_, f32[12,1,4096]{2,1,0:T(1,128)S(1)} %get-tuple-element.11.refs_2_), custom_call_target="tpu_custom_call" | custom-call | tf_op jit(solution)/shard_map/pallas_call | solution.py:748
